TPU v7x, 256 devices: a whole 4x4x8 slice. The times are simulated.
256 devices in a mesh: row: 16 (over y, x), col: 16 (over z, core).
Axes of the slice: x: 4, y: 4, z: 8, core: 2. Of those that a mesh axis runs over, the one named last changes fastest.
Arguments:
- coeffs: bfloat16 [16384, 2048], P('row'), may hold values from -1 to 1
- p_slots: int32 [16, 16, 8], P('row', 'col'), may hold values from 0 to 63, as said below
- p_count: int32 [16, 16], P('row', 'col'), may hold values from 1 to 8
- s_blocks: bfloat16 [16, 16, 8, 128, 128], P('row', 'col'), may hold values from -0.3984375 to 0.3984375
- s_slots: int32 [16, 16, 8], P('row', 'col'), may hold values from 0 to 63, as said below
- s_count: int32 [16, 16], P('row', 'col'), may hold values from 1 to 8
- q_slots: int32 [16, 16, 8], P('row', 'col'), may hold values from 0 to 63, as said below
- q_count: int32 [16, 16], P('row', 'col'), may hold values from 1 to 8
Outputs:
- density: bfloat16 [16, 16, 8, 128, 128], P('row', 'col')
- product: float32 [16, 16, 8, 128, 128], P('row', 'col')
Inputs may be any that keep to these rules, and one draw needn't show every extreme that they name: `p_slots`: on each device the live slots name different blocks of its tile; at least one device has all 8 slots live, which one is drawn. `s_slots`: on each device the live slots name different positions; at least one device has all 8 slots live, which one is drawn. `q_slots`: on each device the live slots name different blocks of its tile; at least one device has all 8 slots live, which one is drawn.
All inputs are finite; a program needn't handle non-finite values.
Results may differ from a plain program's by a relative error of at most 0.0029.
Values may be sent and summed in bfloat16 or wider, within the bound.
A program may use at most 192 MiB of HBM per device.

v0:
```python
import jax
import jax.numpy as jnp
from jax import lax
from jax.sharding import PartitionSpec as P


def from_root(block, axis, source):
    block = jnp.where(lax.axis_index(axis) == source, block, jnp.zeros_like(block))
    return lax.psum(block, axis)


def shortened(shard):

    def short(part):
        return part.astype(jnp.bfloat16) if part.dtype == jnp.float32 else part

    return jax.tree.map(short, shard)


def shifted(block, axis, distance):
    devices = range(lax.axis_size(axis))
    route = [((i - distance) % len(devices), i) for i in devices]
    return lax.ppermute(block, axis, route)


def step_product(summed, p_data, s_data, panel_slot, q_row, q_col, tile_cols):
    p_blocks, p_code = p_data
    s_blocks, s_code = s_data
    local_k = jnp.arange(tile_cols, dtype=jnp.int32)
    p_live = p_code >= 0
    p_row = jnp.where(p_live, p_code // tile_cols, -1)
    p_col = jnp.where(p_live, p_code % tile_cols, -1)
    pick_left = (
        (p_row[:, None, None] == q_row[None, :, None])
        & (p_col[:, None, None] == local_k[None, None, :])
    ).astype(jnp.bfloat16)
    left_rows = jnp.einsum("pqk,pab->qakb", pick_left, p_blocks, preferred_element_type=jnp.float32)
    left_rows = left_rows.astype(jnp.bfloat16).reshape(q_row.shape[0], 128, tile_cols * 128)
    square = tile_cols * tile_cols
    s_live = (s_code >= 0) & (s_code // square == panel_slot)
    s_local = s_code % square
    s_row = jnp.where(s_live, s_local // tile_cols, -1)
    s_col = s_local % tile_cols
    pick_right = (
        (s_row[:, None, None] == local_k[None, :, None])
        & (s_col[:, None, None] == q_col[None, None, :])
    ).astype(jnp.bfloat16)
    right_cols = jnp.einsum(
        "skq,sab->kaqb", pick_right, s_blocks, preferred_element_type=jnp.float32
    )
    right_cols = right_cols.astype(jnp.bfloat16).reshape(tile_cols * 128, q_row.shape[0], 128)
    return summed + jnp.einsum(
        "qak,kqb->qab", left_rows, right_cols, preferred_element_type=jnp.float32
    )


def pick_tree(flag, moved, kept):
    return jax.tree.map(lambda fresh, stale: jnp.where(flag, fresh, stale), moved, kept)


def on_device(coeffs, p_slots, p_count, s_blocks, s_slots, s_count, q_slots, q_count):
    rows_n = lax.axis_size("row")
    cols_n = lax.axis_size("col")
    row_at = lax.axis_index("row")
    col_at = lax.axis_index("col")
    panel_rows, orbitals = coeffs.shape
    tile_rows = panel_rows // 128
    tile_cols = panel_rows * rows_n // cols_n // 128
    sub_span = cols_n // rows_n
    source = from_root(coeffs, "row", col_at // sub_span)
    slot_ids = p_slots[0, 0]
    p_max = slot_ids.shape[0]
    p_live = jnp.arange(p_max, dtype=jnp.int32) < p_count[0, 0]
    left = coeffs.reshape(tile_rows, 128, orbitals)[slot_ids // tile_cols]
    right = source.reshape(tile_cols, 128, orbitals)[slot_ids % tile_cols]
    raw = jnp.einsum("pak,pbk->pab", left, right, preferred_element_type=jnp.float32)
    dense_blocks = jnp.where(p_live[:, None, None], raw, jnp.zeros_like(raw)).astype(jnp.bfloat16)
    p_code = jnp.where(p_live, slot_ids, -1)
    s_ids = s_slots[0, 0]
    s_max = s_ids.shape[0]
    s_live = jnp.arange(s_max, dtype=jnp.int32) < s_count[0, 0]
    s_code = jnp.where(s_live, s_ids, -1)
    s_local = s_blocks[0, 0]
    q_ids = q_slots[0, 0]
    q_max = q_ids.shape[0]
    q_live = jnp.arange(q_max, dtype=jnp.int32) < q_count[0, 0]
    q_row = q_ids // tile_cols
    q_col = q_ids % tile_cols
    zeros_out = jnp.zeros((q_max, 128, 128), jnp.float32)
    p_data = (dense_blocks, p_code)
    s_data = (s_local, s_code)
    level_count = rows_n.bit_length() - 1
    for level in range(level_count):
        moved = jax.tree.map(
            lambda part, own: part.astype(own.dtype),
            shifted(shortened(p_data), "col", -(1 << level)),
            p_data,
        )
        p_data = pick_tree(row_at >> level & 1 == 1, moved, p_data)
    row_offset = col_at % rows_n
    for level in range(level_count):
        moved = jax.tree.map(
            lambda part, own: part.astype(own.dtype),
            shifted(shortened(s_data), "row", -(1 << level)),
            s_data,
        )
        s_data = pick_tree(row_offset >> level & 1 == 1, moved, s_data)

    def advance(step_at, carry):
        summed, p_held, s_held = carry
        panel_at = (row_at + col_at + step_at) % cols_n
        summed = step_product(summed, p_held, s_held, panel_at // rows_n, q_row, q_col, tile_cols)
        p_held = jax.tree.map(
            lambda part, own: part.astype(own.dtype), shifted(shortened(p_held), "col", -1), p_held
        )
        s_held = jax.tree.map(
            lambda part, own: part.astype(own.dtype), shifted(shortened(s_held), "row", -1), s_held
        )
        return (summed, p_held, s_held)

    summed, p_data, s_data = lax.fori_loop(0, cols_n - 1, advance, (zeros_out, p_data, s_data))
    panel_at = (row_at + col_at + cols_n - 1) % cols_n
    summed = step_product(summed, p_data, s_data, panel_at // rows_n, q_row, q_col, tile_cols)
    product = jnp.where(q_live[:, None, None], summed, jnp.zeros_like(summed))
    return (dense_blocks.reshape(1, 1, p_max, 128, 128), product.reshape(1, 1, q_max, 128, 128))


def solution(mesh):
    return jax.shard_map(
        on_device,
        mesh=mesh,
        in_specs=(
            P("row", None),
            P("row", "col", None),
            P("row", "col"),
            P("row", "col", None, None, None),
            P("row", "col", None),
            P("row", "col"),
            P("row", "col", None),
            P("row", "col"),
        ),
        out_specs=(P("row", "col", None, None, None), P("row", "col", None, None, None)),
        check_vma=False,
    )
```

profile of v0, /device:TPU:1, one launch (start us, length us, event | category | flops | bytes accessed | tf_op | source)
XLA Modules:
  0.0 387.4 jit_solution(9958249372721441714)
XLA Ops:
  10.7 5.8 %collective-permute-start.12 = (bf16[8,128,128]{2,0,1:T(8,128)(2,1)S(1)}, bf16[8,128,128]{2,0,1:T(8,128)(2,1)S(1)}, u32[]{:S(2)}, u32[]{:S(2)}) collective-permute-start(bf16[8,128,128]{2,0,1:T(8,128)(2,1)S(1)} %bitcast.134), channel_id=1, source_target_pairs={{16,0},{32,16},{48,32},{64,48},{80,64},{96,80},{112,96},{128,112},... | collective-permute-start | bytes 786440 | tf_op jit(solution)/shard_map/ppermute | solution.py:23
  20.4 5.0 %gather_fusion = bf16[8,128,2048]{2,1,0:T(8,128)(2,1)} fusion(bf16[8,128,2048]{2,1,0:T(8,128)(2,1)} %bitcast.131, s32[1024]{0:T(1024)S(1)} %get-tuple-element.386), kind=kCustom, calls=%fused_computation | custom fusion | bytes 8388640 | tf_op jit(solution)/shard_map/gather | solution.py:74
  25.8 8.4 %collective-permute-start.9 = (s32[8]{0:T(128)S(1)}, s32[8]{0:T(128)S(1)}, u32[]{:S(2)}, u32[]{:S(2)}) collective-permute-start(s32[8]{0:T(128)S(1)} %broadcast_select_fusion.13), channel_id=1, source_target_pairs={{2,0},{3,1},{4,2},{5,3},{6,4},{7,5},{8,6},{9,7},{10,8},{11,9},{12,... | collective-permute-start | bytes 104 | tf_op jit(solution)/shard_map/ppermute | solution.py:23
  36.9 91.7 %all-reduce.2.cloned.1.call-done = bf16[8,128,2048]{2,1,0:T(8,128)(2,1)} async-done(((bf16[8,128,2048]{2,1,0:T(8,128)(2,1)}), bf16[8,128,2048]{2,1,0:T(8,128)(2,1)}) %all-reduce.2.cloned.1.call-update) | async-done | bytes 4194320 | tf_op jit(solution)/shard_map/psum | solution.py:9
  128.6 5.0 %gather_fusion.1 = bf16[8,128,2048]{2,1,0:T(8,128)(2,1)} fusion(bf16[8,128,2048]{2,1,0:T(8,128)(2,1)} %all-reduce.2.cloned.1.call-done, s32[1024]{0:T(1024)S(1)} %get-tuple-element.385), kind=kCustom, calls=%fused_computation.1 | custom fusion | bytes 8388640 | tf_op jit(solution)/shard_map/gather | solution.py:75
  133.6 4.7 %fusion.18 = bf16[8,128,128]{2,1,0:T(8,128)(2,1)S(1)} fusion(bf16[8,128,2048]{2,1,0:T(8,128)(2,1)} %gather_fusion, bf16[8,128,2048]{2,1,0:T(8,128)(2,1)} %gather_fusion.1, pred[8]{0:T(512)(128)(4,1)S(1)} %iota_compare_fusion.5), kind=kOutput, calls=%fused_computation.46 | convolution fusion | flops 537133056 | bytes 8650760 | tf_op jit(solution)/shard_map/pak,pbk->pab/dot_general | solution.py:76
  139.4 2.6 collective-permute-start.19
  142.1 2.3 collective-permute-start.13
  144.6 3.9 %collective-permute-start.5 = (bf16[8,128,128]{2,1,0:T(8,128)(2,1)S(1)}, bf16[8,128,128]{2,1,0:T(8,128)(2,1)S(1)}, u32[]{:S(2)}, u32[]{:S(2)}) collective-permute-start(bf16[8,128,128]{2,1,0:T(8,128)(2,1)S(1)} %broadcast_select_fusion.5), channel_id=1, source_target_pairs={{2,0},{3,1},{4,2},{5,3},{6,4},{7,5},{8,6},{9,7},{10,8},{11,9},{12,... | collective-permute-start | bytes 786440 | tf_op jit(solution)/shard_map/ppermute | solution.py:23
  148.5 3.1 collective-permute-start.11
  151.6 2.7 collective-permute-start.14
  155.6 4.7 %collective-permute-done.14 = bf16[8,128,128]{2,0,1:T(8,128)(2,1)S(1)} collective-permute-done((bf16[8,128,128]{2,0,1:T(8,128)(2,1)S(1)}, bf16[8,128,128]{2,0,1:T(8,128)(2,1)S(1)}, u32[]{:S(2)}, u32[]{:S(2)}) %collective-permute-start.14) | collective-permute-done | bytes 262176 | tf_op jit(solution)/shard_map/ppermute | solution.py:23
  163.6 4.0 %collective-permute-start.7 = (bf16[8,128,128]{2,1,0:T(8,128)(2,1)S(1)}, bf16[8,128,128]{2,1,0:T(8,128)(2,1)S(1)}, u32[]{:S(2)}, u32[]{:S(2)}) collective-permute-start(bf16[8,128,128]{2,1,0:T(8,128)(2,1)S(1)} %broadcast_select_fusion.7), channel_id=1, source_target_pairs={{8,0},{9,1},{10,2},{11,3},{12,4},{13,5},{14,6},{15,7},{0,8},{1,9},... | collective-permute-start | bytes 786440 | tf_op jit(solution)/shard_map/ppermute | solution.py:23
  169.5 9.9 %collective-permute-done.7 = bf16[8,128,128]{2,1,0:T(8,128)(2,1)S(1)} collective-permute-done((bf16[8,128,128]{2,1,0:T(8,128)(2,1)S(1)}, bf16[8,128,128]{2,1,0:T(8,128)(2,1)S(1)}, u32[]{:S(2)}, u32[]{:S(2)}) %collective-permute-start.7) | collective-permute-done | bytes 262176 | tf_op jit(solution)/shard_map/ppermute | solution.py:23
  179.6 191.7 %while.25 = (s32[]{:T(128)}, f32[8,128,128]{2,1,0:T(8,128)}, bf16[8,128,128]{2,0,1:T(8,128)(2,1)S(1)}, s32[8]{0:T(128)S(1)}, bf16[8,128,128]{2,0,1:T(8,128)(2,1)...) while((s32[]{:T(128)}, f32[8,128,128]{2,1,0:T(8,128)}, ...), condition=%wide.region_2.3_spmd.clone, body=%wide.region_1.2_spmd.clone.sunk | while | flops 304351008 | bytes 25692068 | solution.py:121
  181.6 5.7 %collective-permute-start.2 = (bf16[8,128,128]{2,0,1:T(8,128)(2,1)S(1)}, bf16[8,128,128]{2,0,1:T(8,128)(2,1)S(1)}, u32[]{:S(2)}, u32[]{:S(2)}) collective-permute-start(bf16[8,128,128]{2,0,1:T(8,128)(2,1)S(1)} %copy.49), channel_id=1, source_target_pairs={{16,0},{32,16},{48,32},{64,48},{80,64},{96,80},{112,96},{128,112},... | collective-permute-start | bytes 786440 | tf_op jit(solution)/shard_map/while/body/eval_jaxpr/ppermute | solution.py:23
  187.4 4.8 %collective-permute-start.1 = (s32[8]{0:T(128)S(1)}, s32[8]{0:T(128)S(1)}, u32[]{:S(2)}, u32[]{:S(2)}) collective-permute-start(s32[8]{0:T(128)S(1)} %copy.48), channel_id=1, source_target_pairs={{1,0},{2,1},{3,2},{4,3},{5,4},{6,5},{7,6},{8,7},{9,8},{10,9},{11,1... | collective-permute-start | bytes 104 | tf_op jit(solution)/shard_map/while/body/eval_jaxpr/ppermute | solution.py:23
  208.9 2.8 fusion.49
  221.1 2.8 fusion.49
  233.4 2.8 fusion.49
  245.7 2.8 fusion.49
  258.0 2.8 fusion.49
  270.3 2.8 fusion.49
  282.5 2.8 fusion.49
  294.8 2.8 fusion.49
  307.1 2.8 fusion.49
  319.4 2.8 fusion.49
  331.6 2.8 fusion.49
  343.9 2.8 fusion.49
  356.2 2.8 fusion.49
  368.5 2.8 fusion.49
  376.8 2.8 fusion.15
  (422 shorter events, 162.9 us)
Async XLA Ops:
  7.2 121.4 %all-reduce.2.cloned.1.call-start = ((), (), s32[]{:S(2)}) async-start(), calls=%async_computation | async-start | bytes 8388608 | tf_op jit(solution)/shard_map/psum | solution.py:9
  10.7 131.3 %collective-permute-start.12 = (bf16[8,128,128]{2,0,1:T(8,128)(2,1)S(1)}, bf16[8,128,128]{2,0,1:T(8,128)(2,1)S(1)}, u32[]{:S(2)}, u32[]{:S(2)}) collective-permute-start(bf16[8,128,128]{2,0,1:T(8,128)(2,1)S(1)} %bitcast.134), channel_id=1, source_target_pairs={{16,0},{32,16},{48,32},{64,48},{80,64},{96,80},{112,96},{128,112},... | collective-permute-start | bytes 786440 | tf_op jit(solution)/shard_map/ppermute | solution.py:23
  34.2 105.2 %collective-permute-start.18 = (s32[8]{0:T(128)S(1)}, s32[8]{0:T(128)S(1)}, u32[]{:S(2)}, u32[]{:S(2)}) collective-permute-start(s32[8]{0:T(128)S(1)} %broadcast_select_fusion.10), channel_id=1, source_target_pairs={{64,0},{80,16},{96,32},{112,48},{128,64},{144,80},{160,96},{176,11... | collective-permute-start | bytes 104 | tf_op jit(solution)/shard_map/ppermute | solution.py:23
  34.9 113.6 %collective-permute-start.10 = (s32[8]{0:T(128)S(1)}, s32[8]{0:T(128)S(1)}, u32[]{:S(2)}, u32[]{:S(2)}) collective-permute-start(s32[8]{0:T(128)S(1)} %broadcast_select_fusion.14), channel_id=1, source_target_pairs={{4,0},{5,1},{6,2},{7,3},{8,4},{9,5},{10,6},{11,7},{12,8},{13,9},{1... | collective-permute-start | bytes 104 | tf_op jit(solution)/shard_map/ppermute | solution.py:23
  139.4 16.2 %collective-permute-start.19 = (s32[8]{0:T(128)S(1)}, s32[8]{0:T(128)S(1)}, u32[]{:S(2)}, u32[]{:S(2)}) collective-permute-start(s32[8]{0:T(128)S(1)} %broadcast_select_fusion.11), channel_id=1, source_target_pairs={{128,0},{144,16},{160,32},{176,48},{192,64},{208,80},{224,96},{240... | collective-permute-start | bytes 104 | tf_op jit(solution)/shard_map/ppermute | solution.py:23
  148.5 19.0 %collective-permute-start.11 = (s32[8]{0:T(128)S(1)}, s32[8]{0:T(128)S(1)}, u32[]{:S(2)}, u32[]{:S(2)}) collective-permute-start(s32[8]{0:T(128)S(1)} %broadcast_select_fusion.15), channel_id=1, source_target_pairs={{8,0},{9,1},{10,2},{11,3},{12,4},{13,5},{14,6},{15,7},{0,8},{1,9},... | collective-permute-start | bytes 104 | tf_op jit(solution)/shard_map/ppermute | solution.py:23
  163.6 15.8 %collective-permute-start.7 = (bf16[8,128,128]{2,1,0:T(8,128)(2,1)S(1)}, bf16[8,128,128]{2,1,0:T(8,128)(2,1)S(1)}, u32[]{:S(2)}, u32[]{:S(2)}) collective-permute-start(bf16[8,128,128]{2,1,0:T(8,128)(2,1)S(1)} %broadcast_select_fusion.7), channel_id=1, source_target_pairs={{8,0},{9,1},{10,2},{11,3},{12,4},{13,5},{14,6},{15,7},{0,8},{1,9},... | collective-permute-start | bytes 786440 | tf_op jit(solution)/shard_map/ppermute | solution.py:23
  179.7 20.5 %collective-permute-start = (bf16[8,128,128]{2,0,1:T(8,128)(2,1)S(1)}, bf16[8,128,128]{2,0,1:T(8,128)(2,1)S(1)}, u32[]{:S(2)}, u32[]{:S(2)}) collective-permute-start(bf16[8,128,128]{2,0,1:T(8,128)(2,1)S(1)} %copy.47), channel_id=1, source_target_pairs={{1,0},{2,1},{3,2},{4,3},{5,4},{6,5},{7,6},{8,7},{9,8},{10,9},{11,1... | collective-permute-start | bytes 786440 | tf_op jit(solution)/shard_map/while/body/eval_jaxpr/ppermute | solution.py:23
  181.6 18.6 %collective-permute-start.2 = (bf16[8,128,128]{2,0,1:T(8,128)(2,1)S(1)}, bf16[8,128,128]{2,0,1:T(8,128)(2,1)S(1)}, u32[]{:S(2)}, u32[]{:S(2)}) collective-permute-start(bf16[8,128,128]{2,0,1:T(8,128)(2,1)S(1)} %copy.49), channel_id=1, source_target_pairs={{16,0},{32,16},{48,32},{64,48},{80,64},{96,80},{112,96},{128,112},... | collective-permute-start | bytes 786440 | tf_op jit(solution)/shard_map/while/body/eval_jaxpr/ppermute | solution.py:23
  187.4 12.8 %collective-permute-start.1 = (s32[8]{0:T(128)S(1)}, s32[8]{0:T(128)S(1)}, u32[]{:S(2)}, u32[]{:S(2)}) collective-permute-start(s32[8]{0:T(128)S(1)} %copy.48), channel_id=1, source_target_pairs={{1,0},{2,1},{3,2},{4,3},{5,4},{6,5},{7,6},{8,7},{9,8},{10,9},{11,1... | collective-permute-start | bytes 104 | tf_op jit(solution)/shard_map/while/body/eval_jaxpr/ppermute | solution.py:23
  200.3 11.4 %collective-permute-start = (bf16[8,128,128]{2,0,1:T(8,128)(2,1)S(1)}, bf16[8,128,128]{2,0,1:T(8,128)(2,1)S(1)}, u32[]{:S(2)}, u32[]{:S(2)}) collective-permute-start(bf16[8,128,128]{2,0,1:T(8,128)(2,1)S(1)} %copy.47), channel_id=1, source_target_pairs={{1,0},{2,1},{3,2},{4,3},{5,4},{6,5},{7,6},{8,7},{9,8},{10,9},{11,1... | collective-permute-start | bytes 786440 | tf_op jit(solution)/shard_map/while/body/eval_jaxpr/ppermute | solution.py:23
  211.8 12.2 %collective-permute-start = (bf16[8,128,128]{2,0,1:T(8,128)(2,1)S(1)}, bf16[8,128,128]{2,0,1:T(8,128)(2,1)S(1)}, u32[]{:S(2)}, u32[]{:S(2)}) collective-permute-start(bf16[8,128,128]{2,0,1:T(8,128)(2,1)S(1)} %copy.47), channel_id=1, source_target_pairs={{1,0},{2,1},{3,2},{4,3},{5,4},{6,5},{7,6},{8,7},{9,8},{10,9},{11,1... | collective-permute-start | bytes 786440 | tf_op jit(solution)/shard_map/while/body/eval_jaxpr/ppermute | solution.py:23
  224.0 12.2 %collective-permute-start = (bf16[8,128,128]{2,0,1:T(8,128)(2,1)S(1)}, bf16[8,128,128]{2,0,1:T(8,128)(2,1)S(1)}, u32[]{:S(2)}, u32[]{:S(2)}) collective-permute-start(bf16[8,128,128]{2,0,1:T(8,128)(2,1)S(1)} %copy.47), channel_id=1, source_target_pairs={{1,0},{2,1},{3,2},{4,3},{5,4},{6,5},{7,6},{8,7},{9,8},{10,9},{11,1... | collective-permute-start | bytes 786440 | tf_op jit(solution)/shard_map/while/body/eval_jaxpr/ppermute | solution.py:23
  225.1 11.2 %collective-permute-start.2 = (bf16[8,128,128]{2,0,1:T(8,128)(2,1)S(1)}, bf16[8,128,128]{2,0,1:T(8,128)(2,1)S(1)}, u32[]{:S(2)}, u32[]{:S(2)}) collective-permute-start(bf16[8,128,128]{2,0,1:T(8,128)(2,1)S(1)} %copy.49), channel_id=1, source_target_pairs={{16,0},{32,16},{48,32},{64,48},{80,64},{96,80},{112,96},{128,112},... | collective-permute-start | bytes 786440 | tf_op jit(solution)/shard_map/while/body/eval_jaxpr/ppermute | solution.py:23
  236.3 12.2 %collective-permute-start = (bf16[8,128,128]{2,0,1:T(8,128)(2,1)S(1)}, bf16[8,128,128]{2,0,1:T(8,128)(2,1)S(1)}, u32[]{:S(2)}, u32[]{:S(2)}) collective-permute-start(bf16[8,128,128]{2,0,1:T(8,128)(2,1)S(1)} %copy.47), channel_id=1, source_target_pairs={{1,0},{2,1},{3,2},{4,3},{5,4},{6,5},{7,6},{8,7},{9,8},{10,9},{11,1... | collective-permute-start | bytes 786440 | tf_op jit(solution)/shard_map/while/body/eval_jaxpr/ppermute | solution.py:23
  237.3 11.2 %collective-permute-start.2 = (bf16[8,128,128]{2,0,1:T(8,128)(2,1)S(1)}, bf16[8,128,128]{2,0,1:T(8,128)(2,1)S(1)}, u32[]{:S(2)}, u32[]{:S(2)}) collective-permute-start(bf16[8,128,128]{2,0,1:T(8,128)(2,1)S(1)} %copy.49), channel_id=1, source_target_pairs={{16,0},{32,16},{48,32},{64,48},{80,64},{96,80},{112,96},{128,112},... | collective-permute-start | bytes 786440 | tf_op jit(solution)/shard_map/while/body/eval_jaxpr/ppermute | solution.py:23
  248.6 12.2 %collective-permute-start = (bf16[8,128,128]{2,0,1:T(8,128)(2,1)S(1)}, bf16[8,128,128]{2,0,1:T(8,128)(2,1)S(1)}, u32[]{:S(2)}, u32[]{:S(2)}) collective-permute-start(bf16[8,128,128]{2,0,1:T(8,128)(2,1)S(1)} %copy.47), channel_id=1, source_target_pairs={{1,0},{2,1},{3,2},{4,3},{5,4},{6,5},{7,6},{8,7},{9,8},{10,9},{11,1... | collective-permute-start | bytes 786440 | tf_op jit(solution)/shard_map/while/body/eval_jaxpr/ppermute | solution.py:23
  249.6 11.2 %collective-permute-start.2 = (bf16[8,128,128]{2,0,1:T(8,128)(2,1)S(1)}, bf16[8,128,128]{2,0,1:T(8,128)(2,1)S(1)}, u32[]{:S(2)}, u32[]{:S(2)}) collective-permute-start(bf16[8,128,128]{2,0,1:T(8,128)(2,1)S(1)} %copy.49), channel_id=1, source_target_pairs={{16,0},{32,16},{48,32},{64,48},{80,64},{96,80},{112,96},{128,112},... | collective-permute-start | bytes 786440 | tf_op jit(solution)/shard_map/while/body/eval_jaxpr/ppermute | solution.py:23
  260.9 12.2 %collective-permute-start = (bf16[8,128,128]{2,0,1:T(8,128)(2,1)S(1)}, bf16[8,128,128]{2,0,1:T(8,128)(2,1)S(1)}, u32[]{:S(2)}, u32[]{:S(2)}) collective-permute-start(bf16[8,128,128]{2,0,1:T(8,128)(2,1)S(1)} %copy.47), channel_id=1, source_target_pairs={{1,0},{2,1},{3,2},{4,3},{5,4},{6,5},{7,6},{8,7},{9,8},{10,9},{11,1... | collective-permute-start | bytes 786440 | tf_op jit(solution)/shard_map/while/body/eval_jaxpr/ppermute | solution.py:23
  273.1 12.2 %collective-permute-start = (bf16[8,128,128]{2,0,1:T(8,128)(2,1)S(1)}, bf16[8,128,128]{2,0,1:T(8,128)(2,1)S(1)}, u32[]{:S(2)}, u32[]{:S(2)}) collective-permute-start(bf16[8,128,128]{2,0,1:T(8,128)(2,1)S(1)} %copy.47), channel_id=1, source_target_pairs={{1,0},{2,1},{3,2},{4,3},{5,4},{6,5},{7,6},{8,7},{9,8},{10,9},{11,1... | collective-permute-start | bytes 786440 | tf_op jit(solution)/shard_map/while/body/eval_jaxpr/ppermute | solution.py:23
  274.2 11.2 %collective-permute-start.2 = (bf16[8,128,128]{2,0,1:T(8,128)(2,1)S(1)}, bf16[8,128,128]{2,0,1:T(8,128)(2,1)S(1)}, u32[]{:S(2)}, u32[]{:S(2)}) collective-permute-start(bf16[8,128,128]{2,0,1:T(8,128)(2,1)S(1)} %copy.49), channel_id=1, source_target_pairs={{16,0},{32,16},{48,32},{64,48},{80,64},{96,80},{112,96},{128,112},... | collective-permute-start | bytes 786440 | tf_op jit(solution)/shard_map/while/body/eval_jaxpr/ppermute | solution.py:23
  285.4 12.2 %collective-permute-start = (bf16[8,128,128]{2,0,1:T(8,128)(2,1)S(1)}, bf16[8,128,128]{2,0,1:T(8,128)(2,1)S(1)}, u32[]{:S(2)}, u32[]{:S(2)}) collective-permute-start(bf16[8,128,128]{2,0,1:T(8,128)(2,1)S(1)} %copy.47), channel_id=1, source_target_pairs={{1,0},{2,1},{3,2},{4,3},{5,4},{6,5},{7,6},{8,7},{9,8},{10,9},{11,1... | collective-permute-start | bytes 786440 | tf_op jit(solution)/shard_map/while/body/eval_jaxpr/ppermute | solution.py:23
  286.4 11.2 %collective-permute-start.2 = (bf16[8,128,128]{2,0,1:T(8,128)(2,1)S(1)}, bf16[8,128,128]{2,0,1:T(8,128)(2,1)S(1)}, u32[]{:S(2)}, u32[]{:S(2)}) collective-permute-start(bf16[8,128,128]{2,0,1:T(8,128)(2,1)S(1)} %copy.49), channel_id=1, source_target_pairs={{16,0},{32,16},{48,32},{64,48},{80,64},{96,80},{112,96},{128,112},... | collective-permute-start | bytes 786440 | tf_op jit(solution)/shard_map/while/body/eval_jaxpr/ppermute | solution.py:23
  297.7 12.2 %collective-permute-start = (bf16[8,128,128]{2,0,1:T(8,128)(2,1)S(1)}, bf16[8,128,128]{2,0,1:T(8,128)(2,1)S(1)}, u32[]{:S(2)}, u32[]{:S(2)}) collective-permute-start(bf16[8,128,128]{2,0,1:T(8,128)(2,1)S(1)} %copy.47), channel_id=1, source_target_pairs={{1,0},{2,1},{3,2},{4,3},{5,4},{6,5},{7,6},{8,7},{9,8},{10,9},{11,1... | collective-permute-start | bytes 786440 | tf_op jit(solution)/shard_map/while/body/eval_jaxpr/ppermute | solution.py:23
  298.7 11.2 %collective-permute-start.2 = (bf16[8,128,128]{2,0,1:T(8,128)(2,1)S(1)}, bf16[8,128,128]{2,0,1:T(8,128)(2,1)S(1)}, u32[]{:S(2)}, u32[]{:S(2)}) collective-permute-start(bf16[8,128,128]{2,0,1:T(8,128)(2,1)S(1)} %copy.49), channel_id=1, source_target_pairs={{16,0},{32,16},{48,32},{64,48},{80,64},{96,80},{112,96},{128,112},... | collective-permute-start | bytes 786440 | tf_op jit(solution)/shard_map/while/body/eval_jaxpr/ppermute | solution.py:23
  310.0 12.2 %collective-permute-start = (bf16[8,128,128]{2,0,1:T(8,128)(2,1)S(1)}, bf16[8,128,128]{2,0,1:T(8,128)(2,1)S(1)}, u32[]{:S(2)}, u32[]{:S(2)}) collective-permute-start(bf16[8,128,128]{2,0,1:T(8,128)(2,1)S(1)} %copy.47), channel_id=1, source_target_pairs={{1,0},{2,1},{3,2},{4,3},{5,4},{6,5},{7,6},{8,7},{9,8},{10,9},{11,1... | collective-permute-start | bytes 786440 | tf_op jit(solution)/shard_map/while/body/eval_jaxpr/ppermute | solution.py:23
  311.0 11.2 %collective-permute-start.2 = (bf16[8,128,128]{2,0,1:T(8,128)(2,1)S(1)}, bf16[8,128,128]{2,0,1:T(8,128)(2,1)S(1)}, u32[]{:S(2)}, u32[]{:S(2)}) collective-permute-start(bf16[8,128,128]{2,0,1:T(8,128)(2,1)S(1)} %copy.49), channel_id=1, source_target_pairs={{16,0},{32,16},{48,32},{64,48},{80,64},{96,80},{112,96},{128,112},... | collective-permute-start | bytes 786440 | tf_op jit(solution)/shard_map/while/body/eval_jaxpr/ppermute | solution.py:23
  322.2 12.2 %collective-permute-start = (bf16[8,128,128]{2,0,1:T(8,128)(2,1)S(1)}, bf16[8,128,128]{2,0,1:T(8,128)(2,1)S(1)}, u32[]{:S(2)}, u32[]{:S(2)}) collective-permute-start(bf16[8,128,128]{2,0,1:T(8,128)(2,1)S(1)} %copy.47), channel_id=1, source_target_pairs={{1,0},{2,1},{3,2},{4,3},{5,4},{6,5},{7,6},{8,7},{9,8},{10,9},{11,1... | collective-permute-start | bytes 786440 | tf_op jit(solution)/shard_map/while/body/eval_jaxpr/ppermute | solution.py:23
  334.5 12.2 %collective-permute-start = (bf16[8,128,128]{2,0,1:T(8,128)(2,1)S(1)}, bf16[8,128,128]{2,0,1:T(8,128)(2,1)S(1)}, u32[]{:S(2)}, u32[]{:S(2)}) collective-permute-start(bf16[8,128,128]{2,0,1:T(8,128)(2,1)S(1)} %copy.47), channel_id=1, source_target_pairs={{1,0},{2,1},{3,2},{4,3},{5,4},{6,5},{7,6},{8,7},{9,8},{10,9},{11,1... | collective-permute-start | bytes 786440 | tf_op jit(solution)/shard_map/while/body/eval_jaxpr/ppermute | solution.py:23
  335.6 11.2 %collective-permute-start.2 = (bf16[8,128,128]{2,0,1:T(8,128)(2,1)S(1)}, bf16[8,128,128]{2,0,1:T(8,128)(2,1)S(1)}, u32[]{:S(2)}, u32[]{:S(2)}) collective-permute-start(bf16[8,128,128]{2,0,1:T(8,128)(2,1)S(1)} %copy.49), channel_id=1, source_target_pairs={{16,0},{32,16},{48,32},{64,48},{80,64},{96,80},{112,96},{128,112},... | collective-permute-start | bytes 786440 | tf_op jit(solution)/shard_map/while/body/eval_jaxpr/ppermute | solution.py:23
  346.8 12.2 %collective-permute-start = (bf16[8,128,128]{2,0,1:T(8,128)(2,1)S(1)}, bf16[8,128,128]{2,0,1:T(8,128)(2,1)S(1)}, u32[]{:S(2)}, u32[]{:S(2)}) collective-permute-start(bf16[8,128,128]{2,0,1:T(8,128)(2,1)S(1)} %copy.47), channel_id=1, source_target_pairs={{1,0},{2,1},{3,2},{4,3},{5,4},{6,5},{7,6},{8,7},{9,8},{10,9},{11,1... | collective-permute-start | bytes 786440 | tf_op jit(solution)/shard_map/while/body/eval_jaxpr/ppermute | solution.py:23
  359.1 12.2 %collective-permute-start = (bf16[8,128,128]{2,0,1:T(8,128)(2,1)S(1)}, bf16[8,128,128]{2,0,1:T(8,128)(2,1)S(1)}, u32[]{:S(2)}, u32[]{:S(2)}) collective-permute-start(bf16[8,128,128]{2,0,1:T(8,128)(2,1)S(1)} %copy.47), channel_id=1, source_target_pairs={{1,0},{2,1},{3,2},{4,3},{5,4},{6,5},{7,6},{8,7},{9,8},{10,9},{11,1... | collective-permute-start | bytes 786440 | tf_op jit(solution)/shard_map/while/body/eval_jaxpr/ppermute | solution.py:23
  (67 other events, 475.3 us)
Sparse Core Ops, SparseCore 0:
  11.3 117.2 all-reduce.1
where the time goes:
time: 389 us; the launch traced here: 387 us
  starting transfers between devices  119 us (31%)
  waiting for transfers between devices  110 us (28%)
  matrix products  70.5 us (18%)
  local copies, waits for them, and re-layouts  63.9 us (16%)
  between operations  16.2 us (4%)
  other arithmetic  5.74 us (1%)
    ppermute x76, starting transfers between devices, shifted(): return lax.ppermute(block, axis, route)  119 us
    psum x1, waiting for transfers between devices, from_root(): return lax.psum(block, axis)  91.7 us
    dot_general x16, matrix products, step_product(): jnp.einsum('qak,kqb->qab', left_rows, right_cols, preferred_element_type=...  44.2 us
    reshape x16, local copies, waits for them, and re-layouts, step_product(): left_rows.astype(jnp.bfloat16).reshape(q_row.shape[0], 128, tile_cols * 128)  36.8 us
    ppermute x76, waiting for transfers between devices, shifted(): return lax.ppermute(block, axis, route)  18.6 us
    while x90, local copies, waits for them, and re-layouts  14.1 us
    dot_general x16, matrix products, step_product(): jnp.einsum('pqk,pab->qakb', pick_left, p_blocks, preferred_element_type=j...  10.8 us
    dot_general x16, matrix products, step_product(): jnp.einsum('skq,sab->kaqb', pick_right, s_blocks, preferred_element_type=...  10.8 us
  transfers between devices with their start and end apart: 77, of which 7 were waited for; matrix products, arithmetic and copies ran while one was open for 29% of the time, Pallas kernels for 0%

commit v1 on v0

v1 whole, which is shorter than its diff:
```python
import functools

import jax
import jax.numpy as jnp
from jax import lax
from jax.experimental import pallas as pl
from jax.experimental.pallas import tpu as pltpu
from jax.sharding import PartitionSpec as P

MESH = pl.DeviceIdType.MESH
B = 128
OFFSETS = (0, 14, 8, 10, 12, 5, 2, 7, 13, 4, 9, 15, 6, 3, 11, 1)
INVERSE = tuple(OFFSETS.index(o) for o in range(16))


def lookup(table, at):
    value = 0
    for base in range(0, 16, 4):
        packed = sum(table[base + i] << (4 * i) for i in range(4))
        inside = (at // 4 == base // 4).astype(jnp.int32)
        value = value + inside * ((packed // (1 << (4 * (at % 4)))) % 16)
    return value


class Link:
    def __init__(self, send, recv, at):
        self.send, self.recv, self.at = send, recv, at
        self.sent = None

    def start(self, src, dst, device):
        self.sent = pltpu.make_async_remote_copy(
            src_ref=src, dst_ref=dst, send_sem=self.send.at[self.at], recv_sem=self.recv.at[self.at],
            device_id=device, device_id_type=MESH,
        )
        self.sent.start()

    def arrived(self, landing, device):
        pltpu.make_async_remote_copy(
            src_ref=landing, dst_ref=landing, send_sem=self.send.at[self.at], recv_sem=self.recv.at[self.at],
            device_id=device, device_id_type=MESH,
        ).wait_recv()


class PlaneGather:
    def __init__(self, buf, own, send, recv, place):
        self.buf, self.own = buf, own
        self.y, self.x, self.col = place
        self.rows = own.shape[0]
        self.links = [Link(send, recv, m) for m in range(40)]

    def coords(self, half, du, dv):
        if half == 0:
            return (self.y + dv + 4) % 4, (self.x + du + 4) % 4
        return (self.y + du + 4) % 4, (self.x + dv + 4) % 4

    def index(self, half, du, dv):
        y, x = self.coords(half, du, dv)
        return 4 * y + x

    def device(self, half, du, dv):
        return (self.index(half, du, dv), self.col)

    def span(self, half, part):
        size = self.rows // 2
        base = half * size
        if part is None:
            return pl.ds(base, size)
        return pl.ds(base + part * (size // 2), size // 2)

    def block(self, half, du, dv, part=None):
        return self.buf.at[self.index(half, du, dv), self.span(half, part)]

    def link(self, half, number):
        return self.links[20 * half + number]

    def first(self, half):
        src = self.own.at[self.span(half, None)]
        dst = self.block(half, 0, 0)
        self.link(half, 0).start(src, dst, self.device(half, 1, 0))
        self.link(half, 1).start(src, dst, self.device(half, -1, 0))

    def relay_first(self, half, side):
        du = -1 if side == 0 else 1
        self.link(half, side).arrived(self.block(half, du, 0), self.device(half, du, 0))
        part = self.block(half, du, 0, side)
        self.link(half, 2 + side).start(part, part, self.device(half, -du, 0))

    def far_first(self, half):
        for side in range(2):
            part = self.block(half, 2, 0, side)
            self.link(half, 2 + side).arrived(part, self.device(half, -1 if side == 0 else 1, 0))

    def second(self, half, j):
        du = (0, -1, 1, 2)[j]
        dst = self.block(half, du, 0)
        src = self.own.at[self.span(half, None)] if j == 0 else dst
        self.link(half, 4 + 4 * j).start(src, dst, self.device(half, 0, 1))
        self.link(half, 5 + 4 * j).start(src, dst, self.device(half, 0, -1))

    def relay_second(self, half, j, side):
        du = (0, -1, 1, 2)[j]
        dv = -1 if side == 0 else 1
        number = 4 + 4 * j + side
        self.link(half, number).arrived(self.block(half, du, dv), self.device(half, 0, dv))
        part = self.block(half, du, dv, side)
        self.link(half, number + 2).start(part, part, self.device(half, 0, -dv))

    def far_second(self, half, j):
        du = (0, -1, 1, 2)[j]
        for side in range(2):
            part = self.block(half, du, 2, side)
            self.link(half, 6 + 4 * j + side).arrived(part, self.device(half, 0, -1 if side == 0 else 1))

    def finish(self):
        for link in self.links:
            link.sent.wait_send()


def gather_kernel(
    coeffs, sblk, p_slots, p_count, s_slots, s_count, q_slots, q_count,
    dens, pall, sall, sidx,
    own, pan, sown, pcode, scode,
    local_sem, scat_sem, c_send, c_recv, g_send, g_recv, s_send, s_recv, z_send, z_recv,
):
    row = lax.axis_index("row")
    col = lax.axis_index("col")
    y, x = row // 4, row % 4
    z, k = col // 2, col % 2

    load_own = pltpu.make_async_copy(coeffs, own, local_sem.at[0])
    load_s = pltpu.make_async_copy(sblk, sown, local_sem.at[1])
    load_own.start()
    load_s.start()

    serve = 2 * ((z - row // 2 + 8) % 8) + (k + row) % 2
    offset = lookup(OFFSETS, serve)
    dest_row = 4 * ((y + offset // 4) % 4) + (x + offset % 4) % 4
    back = 4 * ((y - col // 4 + 4) % 4) + (x - col % 4 + 4) % 4
    served = lookup(INVERSE, back)
    source_col = 2 * ((col // 2 + served // 2) % 8) + (served + col) % 2
    mine = row == col

    barrier = pltpu.get_barrier_semaphore()
    for j in range(1, 16):
        pl.semaphore_signal(barrier, inc=1, device_id=(row, (col + j) % 16), device_id_type=MESH)
        pl.semaphore_signal(barrier, inc=1, device_id=((row + j) % 16, col), device_id_type=MESH)

    @pl.when(serve != 0)
    def _():
        pl.semaphore_signal(barrier, inc=1, device_id=(dest_row, row), device_id_type=MESH)

    @pl.when(back != 0)
    def _():
        pl.semaphore_signal(barrier, inc=1, device_id=(col, source_col), device_id_type=MESH)

    lane = lax.broadcasted_iota(jnp.int32, (8, B), 1)
    sub = lax.broadcasted_iota(jnp.int32, (8, B), 0)
    pc = jnp.full((8, B), -1, jnp.int32)
    qc = jnp.full((8, B), -100, jnp.int32)
    sc = jnp.full((8, B), -1, jnp.int32)
    p_live = jnp.full((8, B), p_count[0], jnp.int32)
    q_live = jnp.full((8, B), q_count[0], jnp.int32)
    s_live = jnp.full((8, B), s_count[0], jnp.int32)
    for i in range(8):
        pc = jnp.where((lane // 8 == i) & (p_live > i), jnp.full((8, B), p_slots[i], jnp.int32), pc)
        qc = jnp.where(
            (lane % 8 == i) & (lane < 64) & (q_live > i), jnp.full((8, B), q_slots[i], jnp.int32), qc
        )
        sc = jnp.where((sub == i) & (s_live > i), jnp.full((8, B), s_slots[i], jnp.int32), sc)
    pcode[col] = pc
    scode[row] = sc

    load_own.wait()
    load_s.wait()

    @pl.when(serve != 0)
    def _():
        pl.semaphore_wait(barrier, 32)

    @pl.when(serve == 0)
    def _():
        pl.semaphore_wait(barrier, 30)

    def scatter_copy(target_row, device):
        return pltpu.make_async_remote_copy(
            src_ref=own.at[:, :, pl.ds(pl.multiple_of(target_row * B, B), B)],
            dst_ref=pan.at[target_row],
            send_sem=scat_sem.at[0], recv_sem=scat_sem.at[1], device_id=device, device_id_type=MESH,
        )

    @pl.when(serve != 0)
    def _():
        scatter_copy(dest_row, (dest_row, row)).start()

    @pl.when(serve == 0)
    def _():
        pltpu.make_async_copy(
            own.at[:, :, pl.ds(pl.multiple_of(row * B, B), B)], pan.at[row], scat_sem.at[0]
        ).start()

    place = (y, x, col)
    panel = PlaneGather(pan, pan.at[row], c_send, c_recv, place)
    inter = PlaneGather(sall, sown, s_send, s_recv, place)

    for half in range(2):
        inter.first(half)
    keep_s = pltpu.make_async_copy(sown, sall.at[row], local_sem.at[2])
    keep_s.start()

    codes = []
    for j in range(1, 16):
        link = Link(g_send, g_recv, 2 * j - 2)
        link.start(pcode.at[col], pcode.at[col], (row, (col + j) % 16))
        codes.append(link)
        link = Link(g_send, g_recv, 2 * j - 1)
        link.start(scode.at[row], scode.at[row], ((row + j) % 16, col))
        codes.append(link)

    @pl.when(serve != 0)
    def _():
        scatter_copy(row, (col, source_col)).wait_recv()

    @pl.when(serve == 0)
    def _():
        pltpu.make_async_copy(
            own.at[:, :, pl.ds(pl.multiple_of(row * B, B), B)], pan.at[row], scat_sem.at[0]
        ).wait()

    for half in range(2):
        panel.first(half)
    for half in range(2):
        panel.second(half, 0)
    for side in range(2):
        for half in range(2):
            inter.relay_first(half, side)
    for side in range(2):
        for half in range(2):
            panel.relay_first(half, side)
            panel.second(half, 1 + side)
    for half in range(2):
        panel.far_first(half)
        panel.second(half, 3)

    for j in range(1, 16):
        codes[2 * j - 2].arrived(pcode.at[(col - j + 16) % 16], (row, (col - j + 16) % 16))
        codes[2 * j - 1].arrived(scode.at[(row - j + 16) % 16], ((row - j + 16) % 16, col))
    pcs, scs = pcode[...], scode[...]
    q = qc[None]
    match = ((pcs >> 3) == (q >> 3)) & ((scs >> 3) == (pcs & 7)) & ((scs & 7) == (q & 7))
    match = match & (pcs >= 0) & (scs >= 0) & (q >= 0)
    found = jnp.where(match, lax.broadcasted_iota(jnp.int32, (16, 8, B), 1) + 1, 0)
    found = jnp.sum(found, axis=1)
    total = jnp.sum((found > 0).astype(jnp.int32), axis=1, keepdims=True)
    sidx[...] = jnp.where(lax.broadcasted_iota(jnp.int32, (16, B), 1) == 64, total, found)

    for half in range(2):
        inter.far_first(half)
    for j in range(4):
        for side in range(2):
            for half in range(2):
                panel.relay_second(half, j, side)
    for j in range(4):
        for half in range(2):
            panel.far_second(half, j)

    for j in range(4):
        for half in range(2):
            inter.second(half, j)

    for s in range(8):
        a = p_slots[s] >> 3
        b = p_slots[s] & 7
        left = own[a]
        right = jnp.concatenate([pan[i, b] for i in range(16)], axis=1)
        raw = lax.dot_general(left, right, (((1,), (1,)), ((), ())), preferred_element_type=jnp.float32)
        raw = jnp.where(jnp.full((B, B), p_count[0], jnp.int32) > s, raw, 0.0)
        dens[s] = raw.astype(jnp.bfloat16)

    sibling = (row, col + 1 - 2 * k)
    up = (row, (col + 2) % 16)
    down = (row, (col + 14) % 16)
    half_rows = dens.shape[0] // 2
    ring = [Link(z_send, z_recv, m) for m in range(30)]

    def tile(at, chunk):
        return pall.at[at, pl.ds(chunk * half_rows, half_rows)]

    def number(way, distance, chunk):
        return 7 * way + (2 * (distance - 1) + chunk if distance < 4 else 6)

    for chunk in range(2):
        src = dens.at[pl.ds(chunk * half_rows, half_rows)]
        ring[number(0, 1, chunk)].start(src, tile(col, chunk), up)
        ring[number(1, 1, chunk)].start(src, tile(col, chunk), down)
    for chunk in range(2):
        ring[14 + chunk].start(dens.at[pl.ds(chunk * half_rows, half_rows)], tile(col, chunk), sibling)
    keep_p = pltpu.make_async_copy(dens, pall.at[col], local_sem.at[3])
    keep_p.start()

    def pass_on(way, distance, chunk):
        at = (col + 16 - 2 * distance) % 16 if way == 0 else (col + 2 * distance) % 16
        here = tile(at, chunk)
        me = number(way, distance, chunk)
        ring[me].arrived(here, down if way == 0 else up)
        if distance < 3 or (distance == 3 and chunk == way):
            ring[number(way, distance + 1, chunk)].start(here, here, up if way == 0 else down)
        ring[16 + me].start(here, here, sibling)

    def across(me, at, chunk):
        ring[me].arrived(tile(at, chunk), sibling)

    arrivals = [(d, c) for d in (1, 2, 3) for c in range(2)]
    relays = [(j, side) for j in range(4) for side in range(2)]
    for n in range(8):
        if n < 6:
            for way in range(2):
                pass_on(way, *arrivals[n])
        j, side = relays[n]
        for half in range(2):
            inter.relay_second(half, j, side)
    for way in range(2):
        pass_on(way, 4, way)
    for j in range(4):
        for half in range(2):
            inter.far_second(half, j)
    other = col + 1 - 2 * k
    for chunk in range(2):
        across(14 + chunk, other, chunk)
    for way in range(2):
        for distance in (1, 2, 3):
            for chunk in range(2):
                at = (other + 16 - 2 * distance) % 16 if way == 0 else (other + 2 * distance) % 16
                across(16 + number(way, distance, chunk), at, chunk)
        across(16 + number(way, 4, way), (other + 8) % 16, way)

    keep_s.wait()
    keep_p.wait()
    panel.finish()
    inter.finish()
    for link in codes + ring:
        link.sent.wait_send()

    @pl.when(serve != 0)
    def _():
        scatter_copy(dest_row, (dest_row, row)).wait_send()


def product_kernel(sidx, pall, sall, out, todo, pbuf, sbuf, count, sem_p, sem_s):
    depth = pbuf.shape[0]
    out[...] = jnp.zeros_like(out)
    count[0] = 0

    def scan(t, _):
        @pl.when(sidx[t, 64] > 0)
        def _():
            def inner(i, _):
                v = sidx[t, i]

                @pl.when(v > 0)
                def _():
                    n = count[0]
                    todo[n] = t * 1024 + i * 16 + v - 1
                    count[0] = n + 1

                return 0

            lax.fori_loop(0, 64, inner, 0)

        return 0

    lax.fori_loop(0, 16, scan, 0)
    n = count[0]

    def copies(i):
        code = todo[i]
        t, p, s = code // 1024, code // 128 % 8, code % 16
        at = i % depth
        return (
            pltpu.make_async_copy(pall.at[t, p], pbuf.at[at], sem_p.at[at]),
            pltpu.make_async_copy(sall.at[t, s], sbuf.at[at], sem_s.at[at]),
        )

    def begin(i, _):
        for copy in copies(i):
            copy.start()
        return 0

    lax.fori_loop(0, jnp.minimum(n, depth), begin, 0)

    def work(i, _):
        for copy in copies(i):
            copy.wait()
        at = i % depth
        q = todo[i] // 16 % 8
        out[q] += jnp.dot(pbuf[at], sbuf[at], preferred_element_type=jnp.float32)

        @pl.when(i + depth < n)
        def _():
            begin(i + depth, 0)

        return 0

    lax.fori_loop(0, n, work, 0)


def on_device(coeffs, p_slots, p_count, s_blocks, s_slots, s_count, q_slots, q_count):
    rows, orbitals = coeffs.shape
    n = 16
    smem = pl.BlockSpec(memory_space=pltpu.SMEM)
    vmem = pl.BlockSpec(memory_space=pltpu.VMEM)
    anyspace = pl.BlockSpec(memory_space=pl.ANY)
    gathered = jax.ShapeDtypeStruct((n, rows // B, B, B), jnp.bfloat16)
    dma = pltpu.SemaphoreType.DMA
    dens, pall, sall, sidx = pl.pallas_call(
        gather_kernel,
        out_shape=(
            jax.ShapeDtypeStruct((rows // B, B, B), jnp.bfloat16), gathered, gathered,
            jax.ShapeDtypeStruct((n, B), jnp.int32),
        ),
        in_specs=[anyspace, anyspace] + [smem] * 6,
        out_specs=(vmem, anyspace, anyspace, vmem),
        scratch_shapes=[
            pltpu.VMEM((rows // B, B, orbitals), jnp.bfloat16),
            pltpu.VMEM((n, rows // B, B, B), jnp.bfloat16),
            pltpu.VMEM((rows // B, B, B), jnp.bfloat16),
            pltpu.VMEM((n, 8, B), jnp.int32),
            pltpu.VMEM((n, 8, B), jnp.int32),
            dma((4,)), dma((2,)),
            dma((40,)), dma((40,)), dma((30,)), dma((30,)), dma((40,)), dma((40,)), dma((30,)), dma((30,)),
        ],
        compiler_params=pltpu.CompilerParams(collective_id=0, has_side_effects=True),
        name="gather",
    )(
        coeffs.reshape(rows // B, B, orbitals), s_blocks.reshape(rows // B, B, B), p_slots.reshape(8), p_count.reshape(1), s_slots.reshape(8),
        s_count.reshape(1), q_slots.reshape(8), q_count.reshape(1),
    )
    depth = 32
    product = pl.pallas_call(
        product_kernel,
        out_shape=jax.ShapeDtypeStruct((8, B, B), jnp.float32),
        in_specs=[smem, anyspace, anyspace],
        out_specs=vmem,
        scratch_shapes=[
            pltpu.SMEM((1024,), jnp.int32),
            pltpu.VMEM((depth, B, B), jnp.bfloat16),
            pltpu.VMEM((depth, B, B), jnp.bfloat16),
            pltpu.SMEM((1,), jnp.int32),
            dma((depth,)), dma((depth,)),
        ],
        name="product",
    )(sidx, pall, sall)
    return dens.reshape(1, 1, 8, B, B), product.reshape(1, 1, 8, B, B)


def solution(mesh):
    return jax.shard_map(
        on_device,
        mesh=mesh,
        in_specs=(
            P("row", None),
            P("row", "col", None),
            P("row", "col"),
            P("row", "col", None, None, None),
            P("row", "col", None),
            P("row", "col"),
            P("row", "col", None),
            P("row", "col"),
        ),
        out_specs=(P("row", "col", None, None, None), P("row", "col", None, None, None)),
        check_vma=False,
    )
```

time: 389 us -> 104 us (0.27)
  starting transfers between devices: 119 us -> 0 us
  waiting for transfers between devices: 110 us -> 0 us
  Pallas kernels: 0 us -> 99.3 us
  matrix products: 70.5 us -> 0 us
  local copies, waits for them, and re-layouts: 63.9 us -> 0.71 us
  between operations: 16.2 us -> 2.6 us
  other arithmetic: 5.74 us -> 0 us
    ppermute x76 -> x0, starting transfers between devices: 119 us -> none  [shifted(): return lax.ppermute(block, axis, route)]
    pallas_call x0 -> x2, Pallas kernels: none -> 99.3 us  [the longest x1 93.3 us: on_device(): pl.pallas_call(gather_kernel, out_shape=(jax.ShapeDtypeStruct((rows // B,...]
    psum x1 -> x0, waiting for transfers between devices: 91.7 us -> none  [from_root(): return lax.psum(block, axis)]
    dot_general x49 -> x0, matrix products: 70.5 us -> none  [the longest x16 44.2 us: step_product(): jnp.einsum('qak,kqb->qab', left_rows, right_cols, preferred_element_type=...]
    reshape x16 -> x0, local copies, waits for them, and re-layouts: 36.8 us -> none  [step_product(): left_rows.astype(jnp.bfloat16).reshape(q_row.shape[0], 128, tile_cols * 128)]
    ppermute x76 -> x0, waiting for transfers between devices: 18.6 us -> none  [shifted(): return lax.ppermute(block, axis, route)]
    while x90 -> x0, local copies, waits for them, and re-layouts: 14.1 us -> none
    gather x2 -> x0, local copies, waits for them, and re-layouts: 10 us -> none  [the longest x1 5.02 us: on_device(): right = source.reshape(tile_cols, 128, orbitals)[slot_ids % tile_cols]]
  transfers between devices with their start and end apart: 77 -> 0, of which waited for: 7 -> 0; matrix products, arithmetic and copies ran while one was open for 29% -> 0% of each run, Pallas kernels for 0% -> 0%
where the time goes in v1:
time: 104 us; the launch traced here: 103 us
  Pallas kernels  99.3 us (95%)
  between operations  2.6 us (2%)
    pallas_call x1, Pallas kernels, on_device(): pl.pallas_call(gather_kernel, out_shape=(jax.ShapeDtypeStruct((rows // B,...  93.3 us
    pallas_call x1, Pallas kernels, on_device(): pl.pallas_call(product_kernel, out_shape=jax.ShapeDtypeStruct((8, B, B),...  6.07 us

profile of v1, /device:TPU:1, one launch (start us, length us, event | category | flops | bytes accessed | tf_op | source)
XLA Modules:
  0.0 102.6 jit_solution(8052308358485760476)
XLA Ops:
  2.6 93.3 %gather.1 = (bf16[8,128,128]{2,1,0:T(8,128)(2,1)}, bf16[16,8,128,128]{3,2,1,0:T(8,128)(2,1)}, bf16[16,8,128,128]{3,2,1,0:T(8,128)(2,1)}, s32[16,128]{1,0:T(8,128)}) custom-call(bf16[8,128,2048]{2,1,0:T(8,128)(2,1)} %bitcast.13, bf16[8,128,128]{2,1,0:T(8,128)(2,1)} %bitcast.15, s32[8]{0:T(128)} %bitcast.17, s32[1]{0:T(128)} %bitcast.10.p_count, s32[8]{0:T(128)} %bitcast.18, ...), custom_call_target="tpu_custom_call" | custom-call | tf_op jit(solution)/shard_map/gather/pallas_call | solution.py:414
  95.8 0.0 copy-start
  95.8 6.1 %product.1 = f32[8,128,128]{2,1,0:T(8,128)} custom-call(s32[16,128]{1,0:T(8,128)} %get-tuple-element.7.sidx, bf16[16,8,128,128]{3,2,1,0:T(8,128)(2,1)} %get-tuple-element.8.pall, bf16[16,8,128,128]{3,2,1,0:T(8,128)(2,1)} %get-tuple-element.9.sall), custom_call_target="tpu_custom_call" | custom-call | tf_op jit(solution)/shard_map/product/pallas_call | solution.py:438
  101.9 0.0 copy-done
  101.9 0.7 copy.14
Async XLA Ops:
  95.8 6.1 %copy-start = (bf16[8,128,128]{2,1,0:T(8,128)(2,1)S(1)}, bf16[8,128,128]{2,1,0:T(8,128)(2,1)}, u32[]{:S(2)}) copy-start(bf16[8,128,128]{2,1,0:T(8,128)(2,1)} %get-tuple-element.6) | copy-start | bytes 786436

commit v2 on v1

--- a/solution.py
+++ b/solution.py
@@ -9,13 +9,14 @@
 
 MESH = pl.DeviceIdType.MESH
 B = 128
-OFFSETS = (0, 14, 8, 10, 12, 5, 2, 7, 13, 4, 9, 15, 6, 3, 11, 1)
-INVERSE = tuple(OFFSETS.index(o) for o in range(16))
+FIRST = (8, 11, 6, 9, 14, 7, 10, 5)
+SECOND = (2, 1, 12, 3, 4, 13, 0, 15)
+PLANE = tuple((FIRST if i in FIRST else SECOND).index(i) for i in range(16))
 
 
 def lookup(table, at):
     value = 0
-    for base in range(0, 16, 4):
+    for base in range(0, len(table), 4):
         packed = sum(table[base + i] << (4 * i) for i in range(4))
         inside = (at // 4 == base // 4).astype(jnp.int32)
         value = value + inside * ((packed // (1 << (4 * (at % 4)))) % 16)
@@ -118,9 +119,9 @@
 
 def gather_kernel(
     coeffs, sblk, p_slots, p_count, s_slots, s_count, q_slots, q_count,
-    dens, pall, sall, sidx,
-    own, pan, sown, pcode, scode,
-    local_sem, scat_sem, c_send, c_recv, g_send, g_recv, s_send, s_recv, z_send, z_recv,
+    pall, sall, sidx,
+    own, pan, sown, dens, relay, pcode, scode,
+    local_sem, plane_send, plane_recv, far_send, far_recv, c_send, c_recv, g_send, g_recv, s_send, s_recv, z_send, z_recv,
 ):
     row = lax.axis_index("row")
     col = lax.axis_index("col")
@@ -132,26 +133,10 @@
     load_own.start()
     load_s.start()
 
-    serve = 2 * ((z - row // 2 + 8) % 8) + (k + row) % 2
-    offset = lookup(OFFSETS, serve)
-    dest_row = 4 * ((y + offset // 4) % 4) + (x + offset % 4) % 4
-    back = 4 * ((y - col // 4 + 4) % 4) + (x - col % 4 + 4) % 4
-    served = lookup(INVERSE, back)
-    source_col = 2 * ((col // 2 + served // 2) % 8) + (served + col) % 2
-    mine = row == col
-
     barrier = pltpu.get_barrier_semaphore()
     for j in range(1, 16):
         pl.semaphore_signal(barrier, inc=1, device_id=(row, (col + j) % 16), device_id_type=MESH)
         pl.semaphore_signal(barrier, inc=1, device_id=((row + j) % 16, col), device_id_type=MESH)
-
-    @pl.when(serve != 0)
-    def _():
-        pl.semaphore_signal(barrier, inc=1, device_id=(dest_row, row), device_id_type=MESH)
-
-    @pl.when(back != 0)
-    def _():
-        pl.semaphore_signal(barrier, inc=1, device_id=(col, source_col), device_id_type=MESH)
 
     lane = lax.broadcasted_iota(jnp.int32, (8, B), 1)
     sub = lax.broadcasted_iota(jnp.int32, (8, B), 0)
@@ -173,40 +158,75 @@
     load_own.wait()
     load_s.wait()
 
-    @pl.when(serve != 0)
-    def _():
-        pl.semaphore_wait(barrier, 32)
-
-    @pl.when(serve == 0)
-    def _():
-        pl.semaphore_wait(barrier, 30)
-
-    def scatter_copy(target_row, device):
-        return pltpu.make_async_remote_copy(
-            src_ref=own.at[:, :, pl.ds(pl.multiple_of(target_row * B, B), B)],
-            dst_ref=pan.at[target_row],
-            send_sem=scat_sem.at[0], recv_sem=scat_sem.at[1], device_id=device, device_id_type=MESH,
-        )
-
-    @pl.when(serve != 0)
-    def _():
-        scatter_copy(dest_row, (dest_row, row)).start()
-
-    @pl.when(serve == 0)
-    def _():
-        pltpu.make_async_copy(
-            own.at[:, :, pl.ds(pl.multiple_of(row * B, B), B)], pan.at[row], scat_sem.at[0]
-        ).start()
+    pl.semaphore_wait(barrier, 30)
+
+    def slice_of(at):
+        return own.at[pl.ds(4 * k, 4), :, pl.ds(pl.multiple_of(at * B, B), B)]
+
+    class Piece:
+        def __init__(self, e, table):
+            self.shift = lookup(table, z)
+            self.e, self.moves = e, 0 not in table
+            self.peer = row ^ self.shift
+            self.panel = row ^ self.shift
+
+        def copy_in_plane(self):
+            return pltpu.make_async_remote_copy(
+                src_ref=slice_of(self.peer), dst_ref=relay.at[self.e],
+                send_sem=plane_send.at[self.e], recv_sem=plane_recv.at[self.e],
+                device_id=(self.peer, col), device_id_type=MESH,
+            )
+
+        def moved(self, act):
+            if self.moves:
+                act()
+            else:
+                pl.when(self.shift != 0)(act)
+
+        def stays(self, act):
+            if not self.moves:
+                pl.when(self.shift == 0)(act)
+
+        def far(self, src):
+            return pltpu.make_async_remote_copy(
+                src_ref=src, dst_ref=pan.at[row, pl.ds(4 * k, 4)],
+                send_sem=far_send.at[self.e], recv_sem=far_recv.at[k],
+                device_id=(row, self.panel), device_id_type=MESH,
+            )
+
+        def near(self, src):
+            return pltpu.make_async_copy(src, pan.at[row, pl.ds(4 * k, 4)], far_recv.at[k])
+
+        def hand_on(self, src):
+            @pl.when(self.panel == col)
+            def _():
+                self.near(src).start()
+
+            @pl.when(self.panel != col)
+            def _():
+                self.far(src).start()
+
+    pieces = [Piece(0, FIRST), Piece(1, SECOND)]
+    for piece in pieces:
+        piece.moved(lambda piece=piece: piece.copy_in_plane().start())
+        piece.stays(lambda piece=piece: piece.hand_on(slice_of(row)))
 
     place = (y, x, col)
     panel = PlaneGather(pan, pan.at[row], c_send, c_recv, place)
     inter = PlaneGather(sall, sown, s_send, s_recv, place)
+    keep_s = pltpu.make_async_copy(sown, sall.at[row], local_sem.at[2])
+    keep_s.start()
+
+    for piece in pieces:
+
+        def pass_along(piece=piece):
+            piece.copy_in_plane().wait_recv()
+            piece.hand_on(relay.at[piece.e])
+
+        piece.moved(pass_along)
 
     for half in range(2):
         inter.first(half)
-    keep_s = pltpu.make_async_copy(sown, sall.at[row], local_sem.at[2])
-    keep_s.start()
-
     codes = []
     for j in range(1, 16):
         link = Link(g_send, g_recv, 2 * j - 2)
@@ -215,20 +235,26 @@
         link = Link(g_send, g_recv, 2 * j - 1)
         link.start(scode.at[row], scode.at[row], ((row + j) % 16, col))
         codes.append(link)
-
-    @pl.when(serve != 0)
-    def _():
-        scatter_copy(row, (col, source_col)).wait_recv()
-
-    @pl.when(serve == 0)
-    def _():
-        pltpu.make_async_copy(
-            own.at[:, :, pl.ds(pl.multiple_of(row * B, B), B)], pan.at[row], scat_sem.at[0]
-        ).wait()
-
     for half in range(2):
+        inter.second(half, 0)
+
+    my_plane = lookup(PLANE, row ^ col)
+    for half in range(2):
+        landing = pan.at[row, pl.ds(4 * half, 4)]
+        by_me = (my_plane == z) & (k == half)
+
+        @pl.when(by_me)
+        def _(landing=landing, half=half):
+            pltpu.make_async_copy(landing, landing, far_recv.at[half]).wait()
+
+        @pl.when(jnp.logical_not(by_me))
+        def _(landing=landing, half=half):
+            pltpu.make_async_remote_copy(
+                src_ref=landing, dst_ref=landing, send_sem=far_send.at[0], recv_sem=far_recv.at[half],
+                device_id=(row, col + 1 - 2 * k), device_id_type=MESH,
+            ).wait_recv()
+
         panel.first(half)
-    for half in range(2):
         panel.second(half, 0)
     for side in range(2):
         for half in range(2):
@@ -250,8 +276,13 @@
     match = match & (pcs >= 0) & (scs >= 0) & (q >= 0)
     found = jnp.where(match, lax.broadcasted_iota(jnp.int32, (16, 8, B), 1) + 1, 0)
     found = jnp.sum(found, axis=1)
-    total = jnp.sum((found > 0).astype(jnp.int32), axis=1, keepdims=True)
-    sidx[...] = jnp.where(lax.broadcasted_iota(jnp.int32, (16, B), 1) == 64, total, found)
+    source = lax.broadcasted_iota(jnp.int32, (B, B), 0)
+    target = lax.broadcasted_iota(jnp.int32, (B, B), 1)
+    counted = (target == 64 + (source >> 3)) | (target == 72)
+    counts = jnp.dot(
+        (found > 0).astype(jnp.float32), counted.astype(jnp.float32), preferred_element_type=jnp.float32
+    )
+    sidx[...] = jnp.where(lax.broadcasted_iota(jnp.int32, (16, B), 1) < 64, found, counts.astype(jnp.int32))
 
     for half in range(2):
         inter.far_first(half)
@@ -263,7 +294,7 @@
         for half in range(2):
             panel.far_second(half, j)
 
-    for j in range(4):
+    for j in range(1, 4):
         for half in range(2):
             inter.second(half, j)
 
@@ -339,40 +370,22 @@
     inter.finish()
     for link in codes + ring:
         link.sent.wait_send()
-
-    @pl.when(serve != 0)
-    def _():
-        scatter_copy(dest_row, (dest_row, row)).wait_send()
-
-
-def product_kernel(sidx, pall, sall, out, todo, pbuf, sbuf, count, sem_p, sem_s):
+    for piece in pieces:
+        piece.moved(lambda piece=piece: piece.copy_in_plane().wait_send())
+
+        @pl.when(piece.panel != col)
+        def _(piece=piece):
+            piece.far(relay.at[piece.e]).wait_send()
+
+
+def product_kernel(sidx, pall, sall, out, dens, todo, pbuf, sbuf, count, sem, sem_p, sem_s):
     depth = pbuf.shape[0]
-    out[...] = jnp.zeros_like(out)
+    col = lax.axis_index("col")
+    keep = pltpu.make_async_copy(pall.at[col], dens, sem.at[0])
+    keep.start()
     count[0] = 0
 
-    def scan(t, _):
-        @pl.when(sidx[t, 64] > 0)
-        def _():
-            def inner(i, _):
-                v = sidx[t, i]
-
-                @pl.when(v > 0)
-                def _():
-                    n = count[0]
-                    todo[n] = t * 1024 + i * 16 + v - 1
-                    count[0] = n + 1
-
-                return 0
-
-            lax.fori_loop(0, 64, inner, 0)
-
-        return 0
-
-    lax.fori_loop(0, 16, scan, 0)
-    n = count[0]
-
-    def copies(i):
-        code = todo[i]
+    def copies(i, code):
         t, p, s = code // 1024, code // 128 % 8, code % 16
         at = i % depth
         return (
@@ -380,27 +393,60 @@
             pltpu.make_async_copy(sall.at[t, s], sbuf.at[at], sem_s.at[at]),
         )
 
-    def begin(i, _):
-        for copy in copies(i):
+    def begin(i, code):
+        for copy in copies(i, code):
             copy.start()
+
+    def tile(t, _):
+        @pl.when(sidx[t, 72] > 0)
+        def _():
+            def slot(p, _):
+                @pl.when(sidx[t, 64 + p] > 0)
+                def _():
+                    def pair(q, _):
+                        v = sidx[t, 8 * p + q]
+
+                        @pl.when(v > 0)
+                        def _():
+                            n = count[0]
+                            code = t * 1024 + p * 128 + q * 16 + v - 1
+                            todo[n] = code
+                            count[0] = n + 1
+
+                            @pl.when(n < depth)
+                            def _():
+                                begin(n, code)
+
+                        return 0
+
+                    lax.fori_loop(0, 8, pair, 0)
+
+                return 0
+
+            lax.fori_loop(0, 8, slot, 0)
+
         return 0
 
-    lax.fori_loop(0, jnp.minimum(n, depth), begin, 0)
+    lax.fori_loop(0, 16, tile, 0)
+    n = count[0]
+    out[...] = jnp.zeros_like(out)
 
     def work(i, _):
-        for copy in copies(i):
+        code = todo[i]
+        for copy in copies(i, code):
             copy.wait()
         at = i % depth
-        q = todo[i] // 16 % 8
+        q = code // 16 % 8
         out[q] += jnp.dot(pbuf[at], sbuf[at], preferred_element_type=jnp.float32)
 
         @pl.when(i + depth < n)
         def _():
-            begin(i + depth, 0)
+            begin(i + depth, todo[i + depth])
 
         return 0
 
     lax.fori_loop(0, n, work, 0)
+    keep.wait()
 
 
 def on_device(coeffs, p_slots, p_count, s_blocks, s_slots, s_count, q_slots, q_count):
@@ -411,21 +457,22 @@
     anyspace = pl.BlockSpec(memory_space=pl.ANY)
     gathered = jax.ShapeDtypeStruct((n, rows // B, B, B), jnp.bfloat16)
     dma = pltpu.SemaphoreType.DMA
-    dens, pall, sall, sidx = pl.pallas_call(
+    pall, sall, sidx = pl.pallas_call(
         gather_kernel,
         out_shape=(
-            jax.ShapeDtypeStruct((rows // B, B, B), jnp.bfloat16), gathered, gathered,
-            jax.ShapeDtypeStruct((n, B), jnp.int32),
+            gathered, gathered, jax.ShapeDtypeStruct((n, B), jnp.int32),
         ),
         in_specs=[anyspace, anyspace] + [smem] * 6,
-        out_specs=(vmem, anyspace, anyspace, vmem),
+        out_specs=(anyspace, anyspace, vmem),
         scratch_shapes=[
             pltpu.VMEM((rows // B, B, orbitals), jnp.bfloat16),
             pltpu.VMEM((n, rows // B, B, B), jnp.bfloat16),
             pltpu.VMEM((rows // B, B, B), jnp.bfloat16),
+            pltpu.VMEM((rows // B, B, B), jnp.bfloat16),
+            pltpu.VMEM((2, rows // B // 2, B, B), jnp.bfloat16),
             pltpu.VMEM((n, 8, B), jnp.int32),
             pltpu.VMEM((n, 8, B), jnp.int32),
-            dma((4,)), dma((2,)),
+            dma((4,)), dma((2,)), dma((2,)), dma((2,)), dma((2,)),
             dma((40,)), dma((40,)), dma((30,)), dma((30,)), dma((40,)), dma((40,)), dma((30,)), dma((30,)),
         ],
         compiler_params=pltpu.CompilerParams(collective_id=0, has_side_effects=True),
@@ -435,17 +482,19 @@
         s_count.reshape(1), q_slots.reshape(8), q_count.reshape(1),
     )
     depth = 32
-    product = pl.pallas_call(
+    product, dens = pl.pallas_call(
         product_kernel,
-        out_shape=jax.ShapeDtypeStruct((8, B, B), jnp.float32),
+        out_shape=(
+            jax.ShapeDtypeStruct((8, B, B), jnp.float32), jax.ShapeDtypeStruct((8, B, B), jnp.bfloat16)
+        ),
         in_specs=[smem, anyspace, anyspace],
-        out_specs=vmem,
+        out_specs=(vmem, vmem),
         scratch_shapes=[
             pltpu.SMEM((1024,), jnp.int32),
             pltpu.VMEM((depth, B, B), jnp.bfloat16),
             pltpu.VMEM((depth, B, B), jnp.bfloat16),
             pltpu.SMEM((1,), jnp.int32),
-            dma((depth,)), dma((depth,)),
+            dma((1,)), dma((depth,)), dma((depth,)),
         ],
         name="product",
     )(sidx, pall, sall)

time: 104 us -> 91.4 us (0.88); the launches traced: 103 us -> 91.9 us
  Pallas kernels: 99.3 us -> 89.3 us
    pallas_call x2, Pallas kernels: 99.3 us -> 89.3 us  [the longest x1 84.3 us: on_device(): pl.pallas_call(gather_kernel, out_shape=(gathered, gathered, jax.ShapeDty...]
where the time goes in v2:
time: 91.4 us; the launch traced here: 91.9 us
  Pallas kernels  89.3 us (98%)
  between operations  2.58 us (3%)
    pallas_call x1, Pallas kernels, on_device(): pl.pallas_call(gather_kernel, out_shape=(gathered, gathered, jax.ShapeDty...  84.3 us
    pallas_call x1, Pallas kernels, on_device(): pl.pallas_call(product_kernel, out_shape=(jax.ShapeDtypeStruct((8, B, B),...  5 us

profile of v2, /device:TPU:1, one launch (start us, length us, event | category | flops | bytes accessed | tf_op | source)
XLA Modules:
  0.0 91.9 jit_solution(1637231072014130114)
XLA Ops:
  2.6 84.3 %gather.1 = (bf16[16,8,128,128]{3,2,1,0:T(8,128)(2,1)}, bf16[16,8,128,128]{3,2,1,0:T(8,128)(2,1)}, s32[16,128]{1,0:T(8,128)}) custom-call(bf16[8,128,2048]{2,1,0:T(8,128)(2,1)} %bitcast.13, bf16[8,128,128]{2,1,0:T(8,128)(2,1)} %bitcast.14, s32[8]{0:T(128)} %bitcast.15, s32[1]{0:T(128)} %bitcast.10.p_count, s32[8]{0:T(128)} %bitcast.16, s32[1]{0:T(128)} %bitcast.11.s_count, ...), custom_call_target="tpu_custom_call" | custom-call | tf_op jit(solution)/shard_map/gather/pallas_call | solution.py:460
  86.9 5.0 %product.1 = (f32[8,128,128]{2,1,0:T(8,128)}, bf16[8,128,128]{2,1,0:T(8,128)(2,1)}) custom-call(s32[16,128]{1,0:T(8,128)} %get-tuple-element.7.sidx, bf16[16,8,128,128]{3,2,1,0:T(8,128)(2,1)} %get-tuple-element.8.pall, bf16[16,8,128,128]{3,2,1,0:T(8,128)(2,1)} %get-tuple-element.9.sall), custom_call_target="tpu_custom_call" | custom-call | tf_op jit(solution)/shard_map/product/pallas_call | solution.py:485

commit v3 on v2

v3 whole, which is shorter than its diff:
```python
import functools

import jax
import jax.numpy as jnp
from jax import lax
from jax.experimental import pallas as pl
from jax.experimental.pallas import tpu as pltpu
from jax.sharding import PartitionSpec as P

MESH = pl.DeviceIdType.MESH
B = 128
FIRST = (8, 11, 6, 9, 14, 7, 10, 5)
SECOND = (2, 1, 12, 3, 4, 13, 0, 15)
PLANE = tuple((FIRST if i in FIRST else SECOND).index(i) for i in range(16))


def lookup(table, at):
    value = 0
    for base in range(0, len(table), 4):
        packed = sum(table[base + i] << (4 * i) for i in range(4))
        inside = (at // 4 == base // 4).astype(jnp.int32)
        value = value + inside * ((packed // (1 << (4 * (at % 4)))) % 16)
    return value


class Link:
    def __init__(self, send, recv, at):
        self.send, self.recv, self.at = send, recv, at

    def start(self, src, dst, device):
        pltpu.make_async_remote_copy(
            src_ref=src, dst_ref=dst, send_sem=self.send.at[0], recv_sem=self.recv.at[self.at],
            device_id=device, device_id_type=MESH,
        ).start()

    def arrived(self, landing, device):
        pltpu.make_async_remote_copy(
            src_ref=landing, dst_ref=landing, send_sem=self.send.at[0], recv_sem=self.recv.at[self.at],
            device_id=device, device_id_type=MESH,
        ).wait_recv()


def all_sent(send, whole, device):
    pltpu.make_async_remote_copy(
        src_ref=whole, dst_ref=whole, send_sem=send.at[0], recv_sem=send.at[0], device_id=device, device_id_type=MESH
    ).wait_send()


class PlaneGather:
    def __init__(self, buf, own, send, recv, place, streams):
        self.buf, self.own = buf, own
        self.y, self.x, self.col = place
        self.size = own.shape[0] // streams
        self.links = [Link(send, recv, m) for m in range(20 * streams)]

    def index(self, stream, du, dv):
        if stream % 2 == 0:
            return 4 * ((self.y + dv + 4) % 4) + (self.x + du + 4) % 4
        return 4 * ((self.y + du + 4) % 4) + (self.x + dv + 4) % 4

    def device(self, stream, du, dv):
        return (self.index(stream, du, dv), self.col)

    def span(self, stream, part):
        base = (stream % 2) * self.own.shape[0] // 2 + (stream // 2) * self.size
        if part is None:
            return pl.ds(base, self.size)
        return pl.ds(base + part * (self.size // 2), self.size // 2)

    def block(self, stream, du, dv, part=None):
        return self.buf.at[self.index(stream, du, dv), self.span(stream, part)]

    def link(self, stream, number):
        return self.links[20 * stream + number]

    def first(self, stream):
        src = self.own.at[self.span(stream, None)]
        dst = self.block(stream, 0, 0)
        self.link(stream, 0).start(src, dst, self.device(stream, 1, 0))
        self.link(stream, 1).start(src, dst, self.device(stream, -1, 0))

    def relay_first(self, stream, side):
        du = -1 if side == 0 else 1
        self.link(stream, side).arrived(self.block(stream, du, 0), self.device(stream, du, 0))
        part = self.block(stream, du, 0, side)
        self.link(stream, 2 + side).start(part, part, self.device(stream, -du, 0))

    def far_first(self, stream):
        for side in range(2):
            part = self.block(stream, 2, 0, side)
            self.link(stream, 2 + side).arrived(part, self.device(stream, -1 if side == 0 else 1, 0))

    def second(self, stream, j):
        du = (0, -1, 1, 2)[j]
        dst = self.block(stream, du, 0)
        src = self.own.at[self.span(stream, None)] if j == 0 else dst
        self.link(stream, 4 + 4 * j).start(src, dst, self.device(stream, 0, 1))
        self.link(stream, 5 + 4 * j).start(src, dst, self.device(stream, 0, -1))

    def relay_second(self, stream, j, side):
        du = (0, -1, 1, 2)[j]
        dv = -1 if side == 0 else 1
        number = 4 + 4 * j + side
        self.link(stream, number).arrived(self.block(stream, du, dv), self.device(stream, 0, dv))
        part = self.block(stream, du, dv, side)
        self.link(stream, number + 2).start(part, part, self.device(stream, 0, -dv))

    def far_second(self, stream, j):
        du = (0, -1, 1, 2)[j]
        for side in range(2):
            part = self.block(stream, du, 2, side)
            self.link(stream, 6 + 4 * j + side).arrived(part, self.device(stream, 0, -1 if side == 0 else 1))

    def finish(self):
        all_sent(self.links[0].send, self.buf.at[pl.ds(0, 15)], self.device(0, 1, 0))


def gather_kernel(
    coeffs, sblk, p_slots, p_count, s_slots, s_count, q_slots, q_count,
    pall, sall, sidx,
    own, pan, sown, dens, held, relay, code_v, sidx_v,
    local_sem, plane_send, plane_recv, far_send, far_recv, c_send, c_recv, g_send, g_recv, s_send, s_recv, z_send, z_recv,
    x_send, x_recv, keep_sem,
):
    row = lax.axis_index("row")
    col = lax.axis_index("col")
    pcode, scode = code_v.at[pl.ds(0, 16)], code_v.at[pl.ds(16, 16)]
    codes_sent = code_v.at[pl.ds(0, 30)]
    y, x = row // 4, row % 4
    z, k = col // 2, col % 2

    load_own = pltpu.make_async_copy(coeffs, own, local_sem.at[0])
    load_s = pltpu.make_async_copy(sblk, sown, local_sem.at[1])
    load_own.start()
    load_s.start()

    barrier = pltpu.get_barrier_semaphore()
    for j in range(1, 16):
        pl.semaphore_signal(barrier, inc=1, device_id=(row, (col + j) % 16), device_id_type=MESH)
        pl.semaphore_signal(barrier, inc=1, device_id=((row + j) % 16, col), device_id_type=MESH)

    lane = lax.broadcasted_iota(jnp.int32, (8, B), 1)
    sub = lax.broadcasted_iota(jnp.int32, (8, B), 0)
    pc = jnp.full((8, B), -1, jnp.int32)
    qc = jnp.full((8, B), -100, jnp.int32)
    sc = jnp.full((8, B), -1, jnp.int32)
    p_live = jnp.full((8, B), p_count[0], jnp.int32)
    q_live = jnp.full((8, B), q_count[0], jnp.int32)
    s_live = jnp.full((8, B), s_count[0], jnp.int32)
    for i in range(8):
        pc = jnp.where((lane // 8 == i) & (p_live > i), jnp.full((8, B), p_slots[i], jnp.int32), pc)
        qc = jnp.where(
            (lane % 8 == i) & (lane < 64) & (q_live > i), jnp.full((8, B), q_slots[i], jnp.int32), qc
        )
        sc = jnp.where((sub == i) & (s_live > i), jnp.full((8, B), s_slots[i], jnp.int32), sc)
    pcode[col] = pc
    scode[row] = sc

    load_own.wait()
    load_s.wait()

    pl.semaphore_wait(barrier, 30)

    def slice_of(at, chunk):
        return own.at[4 * k + chunk, :, pl.ds(pl.multiple_of(at * B, B), B)]

    class Piece:
        def __init__(self, e, table):
            self.shift = lookup(table, z)
            self.e, self.moves = e, 0 not in table
            self.peer = row ^ self.shift

        def copy_in_plane(self, chunk):
            return pltpu.make_async_remote_copy(
                src_ref=slice_of(self.peer, chunk), dst_ref=relay.at[self.e, chunk],
                send_sem=plane_send.at[self.e, chunk], recv_sem=plane_recv.at[self.e, chunk],
                device_id=(self.peer, col), device_id_type=MESH,
            )

        def moved(self, act):
            if self.moves:
                act()
            else:
                pl.when(self.shift != 0)(act)

        def stays(self, act):
            if not self.moves:
                pl.when(self.shift == 0)(act)

        def far(self, src, chunk):
            return pltpu.make_async_remote_copy(
                src_ref=src, dst_ref=pan.at[row, 4 * k + chunk],
                send_sem=far_send.at[self.e, chunk], recv_sem=far_recv.at[k, chunk],
                device_id=(row, self.peer), device_id_type=MESH,
            )

        def hand_on(self, src, chunk):
            @pl.when(self.peer == col)
            def _():
                pltpu.make_async_copy(src, pan.at[row, 4 * k + chunk], far_recv.at[k, chunk]).start()

            @pl.when(self.peer != col)
            def _():
                self.far(src, chunk).start()

    pieces = [Piece(0, FIRST), Piece(1, SECOND)]
    for chunk in range(4):
        for piece in pieces:
            piece.moved(lambda piece=piece, chunk=chunk: piece.copy_in_plane(chunk).start())
            piece.stays(lambda piece=piece, chunk=chunk: piece.hand_on(slice_of(row, chunk), chunk))

    place = (y, x, col)
    panel = PlaneGather(pan, pan.at[row], c_send, c_recv, place, 4)
    inter = PlaneGather(sall, sown, s_send, s_recv, place, 2)
    keep_s = pltpu.make_async_copy(sown, sall.at[row], local_sem.at[2])
    keep_s.start()

    for chunk in range(4):
        for piece in pieces:

            def pass_along(piece=piece, chunk=chunk):
                piece.copy_in_plane(chunk).wait_recv()
                piece.hand_on(relay.at[piece.e, chunk], chunk)

            piece.moved(pass_along)

    for half in range(2):
        inter.first(half)
    codes = [Link(g_send, g_recv, m) for m in range(8)]

    def code_step(step, act):
        size = 1 << step
        for dim, (ref, me) in enumerate(((pcode, col), (scode, row))):
            mine = me // size * size
            other = me ^ size
            device = (row, other) if dim == 0 else (other, col)
            if act == "start":
                here = ref.at[pl.ds(mine, size)]
                codes[2 * step + dim].start(here, here, device)
            else:
                codes[2 * step + dim].arrived(ref.at[pl.ds(mine ^ size, size)], device)

    code_step(0, "start")

    my_plane = lookup(PLANE, row ^ col)

    def scattered(half, chunk):
        by_me = (my_plane == z) & (k == half)
        landing = pan.at[row, 4 * half + chunk]

        @pl.when(by_me)
        def _():
            pltpu.make_async_copy(landing, landing, far_recv.at[half, chunk]).wait()

        @pl.when(jnp.logical_not(by_me))
        def _():
            pltpu.make_async_remote_copy(
                src_ref=landing, dst_ref=landing, send_sem=far_send.at[0, chunk],
                recv_sem=far_recv.at[half, chunk],
                device_id=(row, col + 1 - 2 * k), device_id_type=MESH,
            ).wait_recv()

    sibling = (row, col + 1 - 2 * k)
    up = (row, (col + 2) % 16)
    down = (row, (col + 14) % 16)
    chunks = 4
    size = dens.shape[0] // chunks
    ring = [Link(z_send, z_recv, m) for m in range(7 * chunks)]
    over = [Link(x_send, x_recv, m) for m in range(8)]

    def number(way, distance, chunk):
        return 7 * chunks // 2 * way + (
            chunks * (distance - 1) + chunk if distance < 4 else 3 * chunks + chunk % (chunks // 2)
        )

    def z_of(way, distance):
        return (z + 8 - distance) % 8 if way == 0 else (z + distance) % 8

    def part(ref, chunk):
        return ref.at[pl.ds(chunk * size, size)]

    def ring_start():
        for chunk in range(chunks):
            for way in range(2):
                ring[number(way, 1, chunk)].start(
                    part(dens, chunk), part(held.at[z], chunk), up if way == 0 else down
                )
        over[0].start(dens, pall.at[col], sibling)
        keep(0).start()

    def keep(slot):
        if slot == 0:
            return pltpu.make_async_copy(dens, pall.at[col], keep_sem.at[0])
        at = z_of(0 if slot < 5 else 1, slot if slot < 5 else slot - 4)
        return pltpu.make_async_copy(held.at[at], pall.at[2 * at + k], keep_sem.at[slot])

    def goes_on(way, distance, chunk):
        return distance < 3 or (distance == 3 and (chunk < chunks // 2) == (way == 0))

    def pass_on(way, distance, chunk):
        here = part(held.at[z_of(way, distance)], chunk)
        ring[number(way, distance, chunk)].arrived(here, down if way == 0 else up)
        if goes_on(way, distance, chunk):
            ring[number(way, distance + 1, chunk)].start(here, here, up if way == 0 else down)
        if distance < 4 and chunk == chunks - 1:
            done(distance if way == 0 else 4 + distance)

    def done(slot):
        at = z_of(0 if slot < 5 else 1, slot if slot < 5 else slot - 4)
        keep(slot).start()
        over[slot].start(held.at[at], pall.at[2 * at + k], sibling)

    def ring_step(distance, chunk):
        for way in range(2):
            if distance < 4 or (chunk < chunks // 2) == (way == 0):
                pass_on(way, distance, chunk)

    steps = [(d, c) for d in (1, 2, 3) for c in range(chunks)] + [
        (4, c) for pair in range(chunks // 2) for c in (pair, pair + chunks // 2)
    ]

    def ring_end():
        for slot in range(8):
            at = z if slot == 0 else z_of(0 if slot < 5 else 1, slot if slot < 5 else slot - 4)
            over[slot].arrived(pall.at[2 * at + 1 - k], sibling)
        for slot in range(8):
            keep(slot).wait()

    def meet():
        code_step(3, "arrived")
        pcs, scs = pcode[...], scode[...]
        q = qc[None]
        match = ((pcs >> 3) == (q >> 3)) & ((scs >> 3) == (pcs & 7)) & ((scs & 7) == (q & 7))
        match = match & (pcs >= 0) & (scs >= 0) & (q >= 0)
        found = jnp.where(match, lax.broadcasted_iota(jnp.int32, (16, 8, B), 1) + 1, 0)
        found = jnp.sum(found, axis=1)
        source = lax.broadcasted_iota(jnp.int32, (B, B), 0)
        target = lax.broadcasted_iota(jnp.int32, (B, B), 1)
        counted = (target == 64 + (source >> 3)) | (target == 72)
        counts = jnp.dot(
            (found > 0).astype(jnp.float32), counted.astype(jnp.float32), preferred_element_type=jnp.float32
        )
        sidx_v[...] = jnp.where(lax.broadcasted_iota(jnp.int32, (16, B), 1) < 64, found, counts.astype(jnp.int32))
        pltpu.make_async_copy(sidx_v, sidx, local_sem.at[3]).start()

    def density():
        for s in range(8):
            a = p_slots[s] >> 3
            b = p_slots[s] & 7
            left = own[a]
            right = jnp.concatenate([pan[i, b] for i in range(16)], axis=1)
            raw = lax.dot_general(left, right, (((1,), (1,)), ((), ())), preferred_element_type=jnp.float32)
            raw = jnp.where(jnp.full((B, B), p_count[0], jnp.int32) > s, raw, 0.0)
            dens[s] = raw.astype(jnp.bfloat16)

    def inter_sends():
        for j in range(4):
            for half in range(2):
                inter.second(half, j)

    relays = [(j, side) for j in range(4) for side in range(2)]

    def inter_step(j, side):
        for half in range(2):
            inter.relay_second(half, j, side)

    def turn(core):
        for wave in range(2):
            for half in range(2):
                for chunk in range(2 * wave, 2 * wave + 2):
                    scattered(half, chunk)
                panel.first(2 * wave + half)
                panel.second(2 * wave + half, 0)
            if wave == 0:
                for side in range(2):
                    for half in range(2):
                        inter.relay_first(half, side)
                code_step(0, "arrived")
                code_step(1, "start")
            for side in range(2):
                for half in range(2):
                    panel.relay_first(2 * wave + half, side)
                    panel.second(2 * wave + half, 1 + side)
            code_step(1 + wave, "arrived")
            code_step(2 + wave, "start")
        for stream in range(4):
            panel.far_first(stream)
            panel.second(stream, 3)
        meet()
        for half in range(2):
            inter.far_first(half)
        for wave in range(2):
            for j in range(4):
                for side in range(2):
                    for half in range(2):
                        panel.relay_second(2 * wave + half, j, side)
        for j in range(4):
            for stream in range(4):
                panel.far_second(stream, j)
        inter_sends()
        density()
        ring_start()
        if True:
            for n, step in enumerate(steps):
                ring_step(*step)
                if 2 <= n < 2 + len(relays):
                    inter_step(*relays[n - 2])
        done(4)
        for j in range(4):
            for half in range(2):
                inter.far_second(half, j)
        ring_end()
        keep_s.wait()
        pltpu.make_async_copy(sidx_v, sidx, local_sem.at[3]).wait()
        panel.finish()
        inter.finish()
        all_sent(g_send, codes_sent, sibling)
        all_sent(z_send, held.at[pl.ds(0, 7)], sibling)
        all_sent(x_send, held, sibling)

    turn(2)

    for chunk in range(4):
        for piece in pieces:
            piece.moved(lambda piece=piece, chunk=chunk: piece.copy_in_plane(chunk).wait_send())

            @pl.when(piece.peer != col)
            def _(piece=piece, chunk=chunk):
                piece.far(relay.at[piece.e, chunk], chunk).wait_send()


def product_kernel(sidx, pall, sall, out, dens, todo, pbuf, sbuf, count, sem, sem_p, sem_s):
    depth = pbuf.shape[0]
    col = lax.axis_index("col")
    keep = pltpu.make_async_copy(pall.at[col], dens, sem.at[0])
    keep.start()
    count[0] = 0

    def copies(i, code):
        t, p, s = code // 1024, code // 128 % 8, code % 16
        at = i % depth
        return (
            pltpu.make_async_copy(pall.at[t, p], pbuf.at[at], sem_p.at[at]),
            pltpu.make_async_copy(sall.at[t, s], sbuf.at[at], sem_s.at[at]),
        )

    def begin(i, code):
        for copy in copies(i, code):
            copy.start()

    def tile(t, _):
        @pl.when(sidx[t, 72] > 0)
        def _():
            def slot(p, _):
                @pl.when(sidx[t, 64 + p] > 0)
                def _():
                    def pair(q, _):
                        v = sidx[t, 8 * p + q]

                        @pl.when(v > 0)
                        def _():
                            n = count[0]
                            code = t * 1024 + p * 128 + q * 16 + v - 1
                            todo[n] = code
                            count[0] = n + 1

                            @pl.when(n < depth)
                            def _():
                                begin(n, code)

                        return 0

                    lax.fori_loop(0, 8, pair, 0)

                return 0

            lax.fori_loop(0, 8, slot, 0)

        return 0

    lax.fori_loop(0, 16, tile, 0)
    n = count[0]
    out[...] = jnp.zeros_like(out)

    def work(i, _):
        code = todo[i]
        for copy in copies(i, code):
            copy.wait()
        at = i % depth
        q = code // 16 % 8
        out[q] += jnp.dot(pbuf[at], sbuf[at], preferred_element_type=jnp.float32)

        @pl.when(i + depth < n)
        def _():
            begin(i + depth, todo[i + depth])

        return 0

    lax.fori_loop(0, n, work, 0)
    keep.wait()


def on_device(coeffs, p_slots, p_count, s_blocks, s_slots, s_count, q_slots, q_count):
    rows, orbitals = coeffs.shape
    n = 16
    smem = pl.BlockSpec(memory_space=pltpu.SMEM)
    vmem = pl.BlockSpec(memory_space=pltpu.VMEM)
    anyspace = pl.BlockSpec(memory_space=pl.ANY)
    gathered = jax.ShapeDtypeStruct((n, rows // B, B, B), jnp.bfloat16)
    dma = pltpu.SemaphoreType.DMA
    pall, sall, sidx = pl.pallas_call(
        gather_kernel,
        out_shape=(
            gathered, gathered, jax.ShapeDtypeStruct((n, B), jnp.int32),
        ),
        in_specs=[anyspace, anyspace] + [smem] * 6,
        out_specs=(anyspace, anyspace, anyspace),
        scratch_shapes=[
            pltpu.VMEM((rows // B, B, orbitals), jnp.bfloat16),
            pltpu.VMEM((n, rows // B, B, B), jnp.bfloat16),
            pltpu.VMEM((rows // B, B, B), jnp.bfloat16),
            pltpu.VMEM((rows // B, B, B), jnp.bfloat16),
            pltpu.VMEM((8, rows // B, B, B), jnp.bfloat16),
            pltpu.VMEM((2, rows // B // 2, B, B), jnp.bfloat16),
            pltpu.VMEM((2 * n, 8, B), jnp.int32),
            pltpu.VMEM((n, B), jnp.int32),
            dma((4,)), dma((2, 4)), dma((2, 4)), dma((2, 4)), dma((2, 4)),
            dma((1,)), dma((80,)), dma((1,)), dma((8,)), dma((1,)), dma((40,)), dma((1,)), dma((28,)),
            dma((1,)), dma((8,)), dma((8,)),
        ],
        compiler_params=pltpu.CompilerParams(collective_id=0, has_side_effects=True),
        name="gather",
    )(
        coeffs.reshape(rows // B, B, orbitals), s_blocks.reshape(rows // B, B, B), p_slots.reshape(8), p_count.reshape(1), s_slots.reshape(8),
        s_count.reshape(1), q_slots.reshape(8), q_count.reshape(1),
    )
    depth = 32
    product, dens = pl.pallas_call(
        product_kernel,
        out_shape=(
            jax.ShapeDtypeStruct((8, B, B), jnp.float32), jax.ShapeDtypeStruct((8, B, B), jnp.bfloat16)
        ),
        in_specs=[smem, anyspace, anyspace],
        out_specs=(vmem, vmem),
        scratch_shapes=[
            pltpu.SMEM((1024,), jnp.int32),
            pltpu.VMEM((depth, B, B), jnp.bfloat16),
            pltpu.VMEM((depth, B, B), jnp.bfloat16),
            pltpu.SMEM((1,), jnp.int32),
            dma((1,)), dma((depth,)), dma((depth,)),
        ],
        name="product",
    )(sidx, pall, sall)
    return dens.reshape(1, 1, 8, B, B), product.reshape(1, 1, 8, B, B)


def solution(mesh):
    return jax.shard_map(
        on_device,
        mesh=mesh,
        in_specs=(
            P("row", None),
            P("row", "col", None),
            P("row", "col"),
            P("row", "col", None, None, None),
            P("row", "col", None),
            P("row", "col"),
            P("row", "col", None),
            P("row", "col"),
        ),
        out_specs=(P("row", "col", None, None, None), P("row", "col", None, None, None)),
        check_vma=False,
    )
```

time: 91.4 us -> 86.1 us (0.942)
  Pallas kernels: 89.3 us -> 83.8 us
    pallas_call x1, Pallas kernels: 84.3 us -> 79.5 us  [on_device(): pl.pallas_call(gather_kernel, out_shape=(gathered, gathered, jax.ShapeDty...]
where the time goes in v3:
time: 86.1 us; the launch traced here: 86.4 us
  Pallas kernels  83.8 us (97%)
  between operations  2.58 us (3%)
    pallas_call x1, Pallas kernels, on_device(): pl.pallas_call(gather_kernel, out_shape=(gathered, gathered, jax.ShapeDty...  79.5 us
    pallas_call x1, Pallas kernels, on_device(): pl.pallas_call(product_kernel, out_shape=(jax.ShapeDtypeStruct((8, B, B),...  4.33 us

profile of v3, /device:TPU:1, one launch (start us, length us, event | category | flops | bytes accessed | tf_op | source)
XLA Modules:
  0.0 86.4 jit_solution(4876210194676793974)
XLA Ops:
  2.6 79.5 %gather.1 = (bf16[16,8,128,128]{3,2,1,0:T(8,128)(2,1)}, bf16[16,8,128,128]{3,2,1,0:T(8,128)(2,1)}, s32[16,128]{1,0:T(8,128)}) custom-call(bf16[8,128,2048]{2,1,0:T(8,128)(2,1)} %bitcast.13, bf16[8,128,128]{2,1,0:T(8,128)(2,1)} %bitcast.14, s32[8]{0:T(128)} %bitcast.15, s32[1]{0:T(128)} %bitcast.10.p_count, s32[8]{0:T(128)} %bitcast.16, s32[1]{0:T(128)} %bitcast.11.s_count, ...), custom_call_target="tpu_custom_call" | custom-call | tf_op jit(solution)/shard_map/gather/pallas_call | solution.py:511
  82.0 4.3 %product.1 = (f32[8,128,128]{2,1,0:T(8,128)}, bf16[8,128,128]{2,1,0:T(8,128)(2,1)}) custom-call(s32[16,128]{1,0:T(8,128)} %get-tuple-element.7.sidx, bf16[16,8,128,128]{3,2,1,0:T(8,128)(2,1)} %get-tuple-element.8.pall, bf16[16,8,128,128]{3,2,1,0:T(8,128)(2,1)} %get-tuple-element.9.sall), custom_call_target="tpu_custom_call" | custom-call | tf_op jit(solution)/shard_map/product/pallas_call | solution.py:538

commit v4 on v3

--- a/solution.py
+++ b/solution.py
@@ -9,6 +9,7 @@
 
 MESH = pl.DeviceIdType.MESH
 B = 128
+LISTED = 128
 FIRST = (8, 11, 6, 9, 14, 7, 10, 5)
 SECOND = (2, 1, 12, 3, 4, 13, 0, 15)
 PLANE = tuple((FIRST if i in FIRST else SECOND).index(i) for i in range(16))
@@ -336,11 +337,40 @@
         found = jnp.sum(found, axis=1)
         source = lax.broadcasted_iota(jnp.int32, (B, B), 0)
         target = lax.broadcasted_iota(jnp.int32, (B, B), 1)
-        counted = (target == 64 + (source >> 3)) | (target == 72)
-        counts = jnp.dot(
-            (found > 0).astype(jnp.float32), counted.astype(jnp.float32), preferred_element_type=jnp.float32
-        )
-        sidx_v[...] = jnp.where(lax.broadcasted_iota(jnp.int32, (16, B), 1) < 64, found, counts.astype(jnp.int32))
+
+        def add_up(left, right):
+            return jnp.dot(
+                left.astype(jnp.bfloat16), right.astype(jnp.bfloat16), preferred_element_type=jnp.float32
+            )
+
+        def flag(condition):
+            return condition.astype(jnp.float32)
+
+        there = flag(found > 0)
+        counts = add_up(there, flag((target == 64 + (source >> 3)) | (target == 72)))
+        lane16 = lax.broadcasted_iota(jnp.int32, (16, B), 1)
+        sidx_v[0:16, :] = jnp.where(lane16 < 64, found, counts.astype(jnp.int32))
+        tile_to = lax.broadcasted_iota(jnp.int32, (16, 16), 0)
+        tile_from = lax.broadcasted_iota(jnp.int32, (16, 16), 1)
+        before = add_up(add_up(flag(tile_from < tile_to), there), flag(source >= 0))
+        spot = before + add_up(there, flag(source <= target)) - 1.0
+        spot = jnp.where((found > 0) & (spot < 128.0), spot, 255.0)
+        spot = lax.dot_general(
+            flag(source == target).astype(jnp.bfloat16), spot.astype(jnp.bfloat16), (((1,), (1,)), ((), ())),
+            preferred_element_type=jnp.float32,
+        ).astype(jnp.int32)
+        tile16 = lax.broadcasted_iota(jnp.int32, (16, B), 0)
+        high = (tile16 * 4 + (lane16 >> 4)).astype(jnp.float32)
+        low = ((lane16 & 15) * 16 + found - 1).astype(jnp.float32)
+        high_sum = jnp.zeros((1, B), jnp.float32)
+        low_sum = jnp.zeros((1, B), jnp.float32)
+        for t in range(16):
+            hit = flag(spot[:, t : t + 1] == target)
+            high_sum += add_up(high[t : t + 1], hit)
+            low_sum += add_up(low[t : t + 1], hit)
+        sidx_v[16:17, :] = high_sum.astype(jnp.int32) * 256 + low_sum.astype(jnp.int32)
+        whole = add_up(flag(tile_from[0:8] >= 0), counts)
+        sidx_v[24:32, :] = whole.astype(jnp.int32)
         pltpu.make_async_copy(sidx_v, sidx, local_sem.at[3]).start()
 
     def density():
@@ -353,11 +383,6 @@
             raw = jnp.where(jnp.full((B, B), p_count[0], jnp.int32) > s, raw, 0.0)
             dens[s] = raw.astype(jnp.bfloat16)
 
-    def inter_sends():
-        for j in range(4):
-            for half in range(2):
-                inter.second(half, j)
-
     relays = [(j, side) for j in range(4) for side in range(2)]
 
     def inter_step(j, side):
@@ -365,46 +390,70 @@
             inter.relay_second(half, j, side)
 
     def turn(core):
-        for wave in range(2):
+        def own(wave):
             for half in range(2):
                 for chunk in range(2 * wave, 2 * wave + 2):
                     scattered(half, chunk)
                 panel.first(2 * wave + half)
                 panel.second(2 * wave + half, 0)
-            if wave == 0:
-                for side in range(2):
-                    for half in range(2):
-                        inter.relay_first(half, side)
-                code_step(0, "arrived")
-                code_step(1, "start")
+
+        def near(wave):
             for side in range(2):
                 for half in range(2):
                     panel.relay_first(2 * wave + half, side)
                     panel.second(2 * wave + half, 1 + side)
-            code_step(1 + wave, "arrived")
-            code_step(2 + wave, "start")
-        for stream in range(4):
-            panel.far_first(stream)
-            panel.second(stream, 3)
-        meet()
-        for half in range(2):
-            inter.far_first(half)
-        for wave in range(2):
-            for j in range(4):
-                for side in range(2):
-                    for half in range(2):
-                        panel.relay_second(2 * wave + half, j, side)
+
+        def far(wave):
+            for half in range(2):
+                panel.far_first(2 * wave + half)
+                panel.second(2 * wave + half, 3)
+
+        def onward(wave, j):
+            for side in range(2):
+                for half in range(2):
+                    panel.relay_second(2 * wave + half, j, side)
+
+        own(0)
+        own(1)
+        near(0)
+        code_step(0, "arrived")
+        code_step(1, "start")
+        onward(0, 0)
+        near(1)
+        code_step(1, "arrived")
+        code_step(2, "start")
+        far(0)
+        onward(0, 1)
+        onward(0, 2)
+        onward(1, 0)
+        far(1)
+        onward(1, 1)
+        onward(1, 2)
+        code_step(2, "arrived")
+        code_step(3, "start")
+        onward(0, 3)
+        onward(1, 3)
         for j in range(4):
             for stream in range(4):
                 panel.far_second(stream, j)
-        inter_sends()
+        for side in range(2):
+            for half in range(2):
+                inter.relay_first(half, side)
+        for j in range(3):
+            for half in range(2):
+                inter.second(half, j)
         density()
         ring_start()
-        if True:
-            for n, step in enumerate(steps):
-                ring_step(*step)
-                if 2 <= n < 2 + len(relays):
-                    inter_step(*relays[n - 2])
+        for n, step in enumerate(steps):
+            ring_step(*step)
+            if n == 0:
+                for half in range(2):
+                    inter.far_first(half)
+                    inter.second(half, 3)
+            if n == 1:
+                meet()
+            if 2 <= n < 2 + len(relays):
+                inter_step(*relays[n - 2])
         done(4)
         for j in range(4):
             for half in range(2):
@@ -434,7 +483,8 @@
     col = lax.axis_index("col")
     keep = pltpu.make_async_copy(pall.at[col], dens, sem.at[0])
     keep.start()
-    count[0] = 0
+    total = sidx[24, 72]
+    count[0] = total
 
     def copies(i, code):
         t, p, s = code // 1024, code // 128 % 8, code % 16
@@ -478,25 +528,47 @@
 
         return 0
 
-    lax.fori_loop(0, 16, tile, 0)
+    def listed(i, _):
+        code = sidx[16, i]
+        todo[i] = code
+
+        @pl.when(i < depth)
+        def _():
+            begin(i, code)
+
+        return 0
+
+    @pl.when(total <= LISTED)
+    def _():
+        lax.fori_loop(0, total, listed, 0)
+
+    @pl.when(total > LISTED)
+    def _():
+        count[0] = 0
+        lax.fori_loop(0, 16, tile, 0)
+
     n = count[0]
     out[...] = jnp.zeros_like(out)
 
-    def work(i, _):
-        code = todo[i]
-        for copy in copies(i, code):
-            copy.wait()
-        at = i % depth
-        q = code // 16 % 8
-        out[q] += jnp.dot(pbuf[at], sbuf[at], preferred_element_type=jnp.float32)
-
-        @pl.when(i + depth < n)
-        def _():
-            begin(i + depth, todo[i + depth])
+    def work(first, size):
+        sums = []
+        for i in [first + g for g in range(size)]:
+            code = todo[i]
+            for copy in copies(i, code):
+                copy.wait()
+            at = i % depth
+            sums.append((code // 16 % 8, jnp.dot(pbuf[at], sbuf[at], preferred_element_type=jnp.float32)))
+        for g, (q, block) in enumerate(sums):
+            out[q] += block
+
+            @pl.when(first + g + depth < n)
+            def _(g=g):
+                begin(first + g + depth, todo[first + g + depth])
 
         return 0
 
-    lax.fori_loop(0, n, work, 0)
+    lax.fori_loop(0, n // 4, lambda i, _: work(4 * i, 4), 0)
+    lax.fori_loop(n // 4 * 4, n, lambda i, _: work(i, 1), 0)
     keep.wait()
 
 
@@ -511,7 +583,7 @@
     pall, sall, sidx = pl.pallas_call(
         gather_kernel,
         out_shape=(
-            gathered, gathered, jax.ShapeDtypeStruct((n, B), jnp.int32),
+            gathered, gathered, jax.ShapeDtypeStruct((2 * n, B), jnp.int32),
         ),
         in_specs=[anyspace, anyspace] + [smem] * 6,
         out_specs=(anyspace, anyspace, anyspace),
@@ -523,7 +595,7 @@
             pltpu.VMEM((8, rows // B, B, B), jnp.bfloat16),
             pltpu.VMEM((2, rows // B // 2, B, B), jnp.bfloat16),
             pltpu.VMEM((2 * n, 8, B), jnp.int32),
-            pltpu.VMEM((n, B), jnp.int32),
+            pltpu.VMEM((2 * n, B), jnp.int32),
             dma((4,)), dma((2, 4)), dma((2, 4)), dma((2, 4)), dma((2, 4)),
             dma((1,)), dma((80,)), dma((1,)), dma((8,)), dma((1,)), dma((40,)), dma((1,)), dma((28,)),
             dma((1,)), dma((8,)), dma((8,)),

time: 86.1 us -> 82.9 us (0.963)
  Pallas kernels: 83.8 us -> 80.4 us
    pallas_call x1, Pallas kernels: 79.5 us -> 76.5 us  [on_device(): pl.pallas_call(gather_kernel, out_shape=(gathered, gathered, jax.ShapeDty...]
where the time goes in v4:
time: 82.9 us; the launch traced here: 83 us
  Pallas kernels  80.4 us (97%)
  between operations  2.58 us (3%)
    pallas_call x1, Pallas kernels, on_device(): pl.pallas_call(gather_kernel, out_shape=(gathered, gathered, jax.ShapeDty...  76.5 us
    pallas_call x1, Pallas kernels, on_device(): pl.pallas_call(product_kernel, out_shape=(jax.ShapeDtypeStruct((8, B, B),...  3.85 us

profile of v4, /device:TPU:1, one launch (start us, length us, event | category | flops | bytes accessed | tf_op | source)
XLA Modules:
  0.0 83.0 jit_solution(10566105734400907226)
XLA Ops:
  2.6 76.5 %gather.1 = (bf16[16,8,128,128]{3,2,1,0:T(8,128)(2,1)}, bf16[16,8,128,128]{3,2,1,0:T(8,128)(2,1)}, s32[32,128]{1,0:T(8,128)}) custom-call(bf16[8,128,2048]{2,1,0:T(8,128)(2,1)} %bitcast.13, bf16[8,128,128]{2,1,0:T(8,128)(2,1)} %bitcast.14, s32[8]{0:T(128)} %bitcast.15, s32[1]{0:T(128)} %bitcast.10.p_count, s32[8]{0:T(128)} %bitcast.16, s32[1]{0:T(128)} %bitcast.11.s_count, ...), custom_call_target="tpu_custom_call" | custom-call | tf_op jit(solution)/shard_map/gather/pallas_call | solution.py:583
  79.1 3.8 %product.1 = (f32[8,128,128]{2,1,0:T(8,128)}, bf16[8,128,128]{2,1,0:T(8,128)(2,1)}) custom-call(s32[32,128]{1,0:T(8,128)} %get-tuple-element.7.sidx, bf16[16,8,128,128]{3,2,1,0:T(8,128)(2,1)} %get-tuple-element.8.pall, bf16[16,8,128,128]{3,2,1,0:T(8,128)(2,1)} %get-tuple-element.9.sall), custom_call_target="tpu_custom_call" | custom-call | tf_op jit(solution)/shard_map/product/pallas_call | solution.py:610

commit v5 on v4

--- a/solution.py
+++ b/solution.py
@@ -52,7 +52,7 @@
         self.buf, self.own = buf, own
         self.y, self.x, self.col = place
         self.size = own.shape[0] // streams
-        self.links = [Link(send, recv, m) for m in range(20 * streams)]
+        self.links = [Link(send, recv, m) for m in range(12 * streams + 1)]
 
     def index(self, stream, du, dv):
         if stream % 2 == 0:
@@ -72,7 +72,7 @@
         return self.buf.at[self.index(stream, du, dv), self.span(stream, part)]
 
     def link(self, stream, number):
-        return self.links[20 * stream + number]
+        return self.links[12 * stream + number]
 
     def first(self, stream):
         src = self.own.at[self.span(stream, None)]
@@ -95,22 +95,19 @@
         du = (0, -1, 1, 2)[j]
         dst = self.block(stream, du, 0)
         src = self.own.at[self.span(stream, None)] if j == 0 else dst
-        self.link(stream, 4 + 4 * j).start(src, dst, self.device(stream, 0, 1))
-        self.link(stream, 5 + 4 * j).start(src, dst, self.device(stream, 0, -1))
+        self.link(stream, 4 + 2 * j).start(src, dst, self.device(stream, 0, 1))
+        self.link(stream, 5 + 2 * j).start(src, dst, self.device(stream, 0, -1))
 
     def relay_second(self, stream, j, side):
         du = (0, -1, 1, 2)[j]
         dv = -1 if side == 0 else 1
-        number = 4 + 4 * j + side
+        number = 4 + 2 * j + side
         self.link(stream, number).arrived(self.block(stream, du, dv), self.device(stream, 0, dv))
         part = self.block(stream, du, dv, side)
-        self.link(stream, number + 2).start(part, part, self.device(stream, 0, -dv))
-
-    def far_second(self, stream, j):
-        du = (0, -1, 1, 2)[j]
-        for side in range(2):
-            part = self.block(stream, du, 2, side)
-            self.link(stream, 6 + 4 * j + side).arrived(part, self.device(stream, 0, -1 if side == 0 else 1))
+        self.links[-1].start(part, part, self.device(stream, 0, -dv))
+
+    def far_second(self):
+        self.links[-1].arrived(self.buf.at[pl.ds(0, 4)], self.device(0, 0, 1))
 
     def finish(self):
         all_sent(self.links[0].send, self.buf.at[pl.ds(0, 15)], self.device(0, 1, 0))
@@ -174,7 +171,7 @@
         def copy_in_plane(self, chunk):
             return pltpu.make_async_remote_copy(
                 src_ref=slice_of(self.peer, chunk), dst_ref=relay.at[self.e, chunk],
-                send_sem=plane_send.at[self.e, chunk], recv_sem=plane_recv.at[self.e, chunk],
+                send_sem=plane_send.at[self.e], recv_sem=plane_recv.at[self.e, chunk],
                 device_id=(self.peer, col), device_id_type=MESH,
             )
 
@@ -191,7 +188,7 @@
         def far(self, src, chunk):
             return pltpu.make_async_remote_copy(
                 src_ref=src, dst_ref=pan.at[row, 4 * k + chunk],
-                send_sem=far_send.at[self.e, chunk], recv_sem=far_recv.at[k, chunk],
+                send_sem=far_send.at[self.e], recv_sem=far_recv.at[k, chunk],
                 device_id=(row, self.peer), device_id_type=MESH,
             )
 
@@ -256,7 +253,7 @@
         @pl.when(jnp.logical_not(by_me))
         def _():
             pltpu.make_async_remote_copy(
-                src_ref=landing, dst_ref=landing, send_sem=far_send.at[0, chunk],
+                src_ref=landing, dst_ref=landing, send_sem=far_send.at[0],
                 recv_sem=far_recv.at[half, chunk],
                 device_id=(row, col + 1 - 2 * k), device_id_type=MESH,
             ).wait_recv()
@@ -267,7 +264,7 @@
     chunks = 4
     size = dens.shape[0] // chunks
     ring = [Link(z_send, z_recv, m) for m in range(7 * chunks)]
-    over = [Link(x_send, x_recv, m) for m in range(8)]
+    over = Link(x_send, x_recv, 0)
 
     def number(way, distance, chunk):
         return 7 * chunks // 2 * way + (
@@ -280,20 +277,17 @@
     def part(ref, chunk):
         return ref.at[pl.ds(chunk * size, size)]
 
-    def ring_start():
-        for chunk in range(chunks):
-            for way in range(2):
-                ring[number(way, 1, chunk)].start(
-                    part(dens, chunk), part(held.at[z], chunk), up if way == 0 else down
-                )
-        over[0].start(dens, pall.at[col], sibling)
-        keep(0).start()
-
-    def keep(slot):
-        if slot == 0:
-            return pltpu.make_async_copy(dens, pall.at[col], keep_sem.at[0])
-        at = z_of(0 if slot < 5 else 1, slot if slot < 5 else slot - 4)
-        return pltpu.make_async_copy(held.at[at], pall.at[2 * at + k], keep_sem.at[slot])
+    def ring_start(chunk):
+        for way in range(2):
+            ring[number(way, 1, chunk)].start(
+                part(dens, chunk), part(held.at[z], chunk), up if way == 0 else down
+            )
+
+    def share(at, first, count):
+        src = (dens if at is None else held.at[at]).at[pl.ds(first, count)]
+        dst = pall.at[col if at is None else 2 * at + k, pl.ds(first, count)]
+        pltpu.make_async_copy(src, dst, keep_sem.at[0]).start()
+        over.start(src, dst, sibling)
 
     def goes_on(way, distance, chunk):
         return distance < 3 or (distance == 3 and (chunk < chunks // 2) == (way == 0))
@@ -304,12 +298,9 @@
         if goes_on(way, distance, chunk):
             ring[number(way, distance + 1, chunk)].start(here, here, up if way == 0 else down)
         if distance < 4 and chunk == chunks - 1:
-            done(distance if way == 0 else 4 + distance)
-
-    def done(slot):
-        at = z_of(0 if slot < 5 else 1, slot if slot < 5 else slot - 4)
-        keep(slot).start()
-        over[slot].start(held.at[at], pall.at[2 * at + k], sibling)
+            share(z_of(way, distance), 0, dens.shape[0])
+        if distance == 4 and chunk % (chunks // 2) == chunks // 2 - 1:
+            share(z_of(way, 4), way * (dens.shape[0] // 2), dens.shape[0] // 2)
 
     def ring_step(distance, chunk):
         for way in range(2):
@@ -321,11 +312,8 @@
     ]
 
     def ring_end():
-        for slot in range(8):
-            at = z if slot == 0 else z_of(0 if slot < 5 else 1, slot if slot < 5 else slot - 4)
-            over[slot].arrived(pall.at[2 * at + 1 - k], sibling)
-        for slot in range(8):
-            keep(slot).wait()
+        over.arrived(pall.at[pl.ds(0, 8)], sibling)
+        pltpu.make_async_copy(held, pall.at[pl.ds(0, 8)], keep_sem.at[0]).wait()
 
     def meet():
         code_step(3, "arrived")
@@ -382,6 +370,10 @@
             raw = lax.dot_general(left, right, (((1,), (1,)), ((), ())), preferred_element_type=jnp.float32)
             raw = jnp.where(jnp.full((B, B), p_count[0], jnp.int32) > s, raw, 0.0)
             dens[s] = raw.astype(jnp.bfloat16)
+            if s % size == size - 1 and s >= size:
+                ring_start(s // size - 1)
+        ring_start(chunks - 1)
+        share(None, 0, dens.shape[0])
 
     relays = [(j, side) for j in range(4) for side in range(2)]
 
@@ -433,9 +425,7 @@
         code_step(3, "start")
         onward(0, 3)
         onward(1, 3)
-        for j in range(4):
-            for stream in range(4):
-                panel.far_second(stream, j)
+        panel.far_second()
         for side in range(2):
             for half in range(2):
                 inter.relay_first(half, side)
@@ -443,7 +433,6 @@
             for half in range(2):
                 inter.second(half, j)
         density()
-        ring_start()
         for n, step in enumerate(steps):
             ring_step(*step)
             if n == 0:
@@ -454,10 +443,7 @@
                 meet()
             if 2 <= n < 2 + len(relays):
                 inter_step(*relays[n - 2])
-        done(4)
-        for j in range(4):
-            for half in range(2):
-                inter.far_second(half, j)
+        inter.far_second()
         ring_end()
         keep_s.wait()
         pltpu.make_async_copy(sidx_v, sidx, local_sem.at[3]).wait()
@@ -469,13 +455,17 @@
 
     turn(2)
 
-    for chunk in range(4):
-        for piece in pieces:
-            piece.moved(lambda piece=piece, chunk=chunk: piece.copy_in_plane(chunk).wait_send())
-
-            @pl.when(piece.peer != col)
-            def _(piece=piece, chunk=chunk):
-                piece.far(relay.at[piece.e, chunk], chunk).wait_send()
+    for piece in pieces:
+
+        def left(sems, piece=piece):
+            whole = relay.at[piece.e]
+            pltpu.make_async_remote_copy(
+                src_ref=whole, dst_ref=whole, send_sem=sems.at[piece.e], recv_sem=sems.at[piece.e],
+                device_id=sibling, device_id_type=MESH,
+            ).wait_send()
+
+        piece.moved(functools.partial(left, plane_send))
+        pl.when(piece.peer != col)(functools.partial(left, far_send))
 
 
 def product_kernel(sidx, pall, sall, out, dens, todo, pbuf, sbuf, count, sem, sem_p, sem_s):
@@ -596,9 +586,9 @@
             pltpu.VMEM((2, rows // B // 2, B, B), jnp.bfloat16),
             pltpu.VMEM((2 * n, 8, B), jnp.int32),
             pltpu.VMEM((2 * n, B), jnp.int32),
-            dma((4,)), dma((2, 4)), dma((2, 4)), dma((2, 4)), dma((2, 4)),
-            dma((1,)), dma((80,)), dma((1,)), dma((8,)), dma((1,)), dma((40,)), dma((1,)), dma((28,)),
-            dma((1,)), dma((8,)), dma((8,)),
+            dma((4,)), dma((2,)), dma((2, 4)), dma((2,)), dma((2, 4)),
+            dma((1,)), dma((49,)), dma((1,)), dma((8,)), dma((1,)), dma((25,)), dma((1,)), dma((28,)),
+            dma((1,)), dma((1,)), dma((1,)),
         ],
         compiler_params=pltpu.CompilerParams(collective_id=0, has_side_effects=True),
         name="gather",

time: 82.9 us -> 81.5 us (0.983)
  Pallas kernels: 80.4 us -> 79 us
    pallas_call x1, Pallas kernels: 76.5 us -> 75.1 us  [on_device(): pl.pallas_call(gather_kernel, out_shape=(gathered, gathered, jax.ShapeDty...]
where the time goes in v5:
time: 81.5 us
  Pallas kernels  79 us (97%)
  between operations  2.58 us (3%)
    pallas_call x1, Pallas kernels, on_device(): pl.pallas_call(gather_kernel, out_shape=(gathered, gathered, jax.ShapeDty...  75.1 us
    pallas_call x1, Pallas kernels, on_device(): pl.pallas_call(product_kernel, out_shape=(jax.ShapeDtypeStruct((8, B, B),...  3.85 us

profile of v5, /device:TPU:1, one launch (start us, length us, event | category | flops | bytes accessed | tf_op | source)
XLA Modules:
  0.0 81.5 jit_solution(6803565161621166957)
XLA Ops:
  2.6 75.1 %gather.1 = (bf16[16,8,128,128]{3,2,1,0:T(8,128)(2,1)}, bf16[16,8,128,128]{3,2,1,0:T(8,128)(2,1)}, s32[32,128]{1,0:T(8,128)}) custom-call(bf16[8,128,2048]{2,1,0:T(8,128)(2,1)} %bitcast.13, bf16[8,128,128]{2,1,0:T(8,128)(2,1)} %bitcast.14, s32[8]{0:T(128)} %bitcast.15, s32[1]{0:T(128)} %bitcast.10.p_count, s32[8]{0:T(128)} %bitcast.16, s32[1]{0:T(128)} %bitcast.11.s_count, ...), custom_call_target="tpu_custom_call" | custom-call | tf_op jit(solution)/shard_map/gather/pallas_call | solution.py:573
  77.7 3.8 %product.1 = (f32[8,128,128]{2,1,0:T(8,128)}, bf16[8,128,128]{2,1,0:T(8,128)(2,1)}) custom-call(s32[32,128]{1,0:T(8,128)} %get-tuple-element.7.sidx, bf16[16,8,128,128]{3,2,1,0:T(8,128)(2,1)} %get-tuple-element.8.pall, bf16[16,8,128,128]{3,2,1,0:T(8,128)(2,1)} %get-tuple-element.9.sall), custom_call_target="tpu_custom_call" | custom-call | tf_op jit(solution)/shard_map/product/pallas_call | solution.py:600

commit v6 on v5

--- a/solution.py
+++ b/solution.py
@@ -114,11 +114,12 @@
 
 
 def gather_kernel(
-    coeffs, sblk, p_slots, p_count, s_slots, s_count, q_slots, q_count,
-    pall, sall, sidx,
-    own, pan, sown, dens, held, relay, code_v, sidx_v,
+    coeffs, sblk, p_slots_in, p_count_in, s_slots_in, s_count_in, q_slots_in, q_count_in,
+    pall, sall, pairs, table,
+    p_slots, p_count, s_slots, s_count, q_slots, q_count,
+    own, pan, sown, dens, held, relay, code_v, pairs_v, table_v,
     local_sem, plane_send, plane_recv, far_send, far_recv, c_send, c_recv, g_send, g_recv, s_send, s_recv, z_send, z_recv,
-    x_send, x_recv, keep_sem,
+    x_send, x_recv, keep_sem, small_sem,
 ):
     row = lax.axis_index("row")
     col = lax.axis_index("col")
@@ -129,13 +130,25 @@
 
     load_own = pltpu.make_async_copy(coeffs, own, local_sem.at[0])
     load_s = pltpu.make_async_copy(sblk, sown, local_sem.at[1])
-    load_own.start()
-    load_s.start()
 
     barrier = pltpu.get_barrier_semaphore()
     for j in range(1, 16):
         pl.semaphore_signal(barrier, inc=1, device_id=(row, (col + j) % 16), device_id_type=MESH)
         pl.semaphore_signal(barrier, inc=1, device_id=((row + j) % 16, col), device_id_type=MESH)
+
+    load_own.start()
+    load_s.start()
+    small = [
+        pltpu.make_async_copy(src, dst, small_sem.at[at])
+        for at, (src, dst) in enumerate((
+            (p_slots_in, p_slots), (p_count_in, p_count), (s_slots_in, s_slots),
+            (s_count_in, s_count), (q_slots_in, q_slots), (q_count_in, q_count),
+        ))
+    ]
+    for copy in small:
+        copy.start()
+    for copy in small:
+        copy.wait()
 
     lane = lax.broadcasted_iota(jnp.int32, (8, B), 1)
     sub = lax.broadcasted_iota(jnp.int32, (8, B), 0)
@@ -337,7 +350,7 @@
         there = flag(found > 0)
         counts = add_up(there, flag((target == 64 + (source >> 3)) | (target == 72)))
         lane16 = lax.broadcasted_iota(jnp.int32, (16, B), 1)
-        sidx_v[0:16, :] = jnp.where(lane16 < 64, found, counts.astype(jnp.int32))
+        table_v[...] = jnp.where(lane16 < 64, found, counts.astype(jnp.int32))
         tile_to = lax.broadcasted_iota(jnp.int32, (16, 16), 0)
         tile_from = lax.broadcasted_iota(jnp.int32, (16, 16), 1)
         before = add_up(add_up(flag(tile_from < tile_to), there), flag(source >= 0))
@@ -356,10 +369,10 @@
             hit = flag(spot[:, t : t + 1] == target)
             high_sum += add_up(high[t : t + 1], hit)
             low_sum += add_up(low[t : t + 1], hit)
-        sidx_v[16:17, :] = high_sum.astype(jnp.int32) * 256 + low_sum.astype(jnp.int32)
-        whole = add_up(flag(tile_from[0:8] >= 0), counts)
-        sidx_v[24:32, :] = whole.astype(jnp.int32)
-        pltpu.make_async_copy(sidx_v, sidx, local_sem.at[3]).start()
+        pairs_v[0:1, :] = high_sum.astype(jnp.int32) * 256 + low_sum.astype(jnp.int32)
+        pairs_v[1:2, :] = add_up(flag(tile_from[0:8] >= 0), counts)[0:1].astype(jnp.int32)
+        pltpu.make_async_copy(table_v, table, local_sem.at[3]).start()
+        pltpu.make_async_copy(pairs_v, pairs, local_sem.at[4]).start()
 
     def density():
         for s in range(8):
@@ -446,7 +459,8 @@
         inter.far_second()
         ring_end()
         keep_s.wait()
-        pltpu.make_async_copy(sidx_v, sidx, local_sem.at[3]).wait()
+        pltpu.make_async_copy(table_v, table, local_sem.at[3]).wait()
+        pltpu.make_async_copy(pairs_v, pairs, local_sem.at[4]).wait()
         panel.finish()
         inter.finish()
         all_sent(g_send, codes_sent, sibling)
@@ -468,12 +482,12 @@
         pl.when(piece.peer != col)(functools.partial(left, far_send))
 
 
-def product_kernel(sidx, pall, sall, out, dens, todo, pbuf, sbuf, count, sem, sem_p, sem_s):
+def product_kernel(pairs, table, pall, sall, out, dens, sidx, todo, pbuf, sbuf, count, sem, sem_p, sem_s):
     depth = pbuf.shape[0]
     col = lax.axis_index("col")
     keep = pltpu.make_async_copy(pall.at[col], dens, sem.at[0])
     keep.start()
-    total = sidx[24, 72]
+    total = pairs[1, 72]
     count[0] = total
 
     def copies(i, code):
@@ -519,7 +533,7 @@
         return 0
 
     def listed(i, _):
-        code = sidx[16, i]
+        code = pairs[0, i]
         todo[i] = code
 
         @pl.when(i < depth)
@@ -534,6 +548,9 @@
 
     @pl.when(total > LISTED)
     def _():
+        fetch = pltpu.make_async_copy(table, sidx, sem.at[1])
+        fetch.start()
+        fetch.wait()
         count[0] = 0
         lax.fori_loop(0, 16, tile, 0)
 
@@ -570,14 +587,15 @@
     anyspace = pl.BlockSpec(memory_space=pl.ANY)
     gathered = jax.ShapeDtypeStruct((n, rows // B, B, B), jnp.bfloat16)
     dma = pltpu.SemaphoreType.DMA
-    pall, sall, sidx = pl.pallas_call(
+    pall, sall, pairs, table = pl.pallas_call(
         gather_kernel,
         out_shape=(
-            gathered, gathered, jax.ShapeDtypeStruct((2 * n, B), jnp.int32),
+            gathered, gathered, jax.ShapeDtypeStruct((8, B), jnp.int32), jax.ShapeDtypeStruct((n, B), jnp.int32),
         ),
-        in_specs=[anyspace, anyspace] + [smem] * 6,
-        out_specs=(anyspace, anyspace, anyspace),
+        in_specs=[anyspace] * 8,
+        out_specs=(anyspace, anyspace, anyspace, anyspace),
         scratch_shapes=[
+            *[pltpu.SMEM((size,), jnp.int32) for size in (8, 1) * 3],
             pltpu.VMEM((rows // B, B, orbitals), jnp.bfloat16),
             pltpu.VMEM((n, rows // B, B, B), jnp.bfloat16),
             pltpu.VMEM((rows // B, B, B), jnp.bfloat16),
@@ -585,10 +603,11 @@
             pltpu.VMEM((8, rows // B, B, B), jnp.bfloat16),
             pltpu.VMEM((2, rows // B // 2, B, B), jnp.bfloat16),
             pltpu.VMEM((2 * n, 8, B), jnp.int32),
-            pltpu.VMEM((2 * n, B), jnp.int32),
-            dma((4,)), dma((2,)), dma((2, 4)), dma((2,)), dma((2, 4)),
+            pltpu.VMEM((8, B), jnp.int32),
+            pltpu.VMEM((n, B), jnp.int32),
+            dma((5,)), dma((2,)), dma((2, 4)), dma((2,)), dma((2, 4)),
             dma((1,)), dma((49,)), dma((1,)), dma((8,)), dma((1,)), dma((25,)), dma((1,)), dma((28,)),
-            dma((1,)), dma((1,)), dma((1,)),
+            dma((1,)), dma((1,)), dma((1,)), dma((6,)),
         ],
         compiler_params=pltpu.CompilerParams(collective_id=0, has_side_effects=True),
         name="gather",
@@ -602,17 +621,18 @@
         out_shape=(
             jax.ShapeDtypeStruct((8, B, B), jnp.float32), jax.ShapeDtypeStruct((8, B, B), jnp.bfloat16)
         ),
-        in_specs=[smem, anyspace, anyspace],
+        in_specs=[smem, anyspace, anyspace, anyspace],
         out_specs=(vmem, vmem),
         scratch_shapes=[
+            pltpu.SMEM((n, B), jnp.int32),
             pltpu.SMEM((1024,), jnp.int32),
             pltpu.VMEM((depth, B, B), jnp.bfloat16),
             pltpu.VMEM((depth, B, B), jnp.bfloat16),
             pltpu.SMEM((1,), jnp.int32),
-            dma((1,)), dma((depth,)), dma((depth,)),
+            dma((2,)), dma((depth,)), dma((depth,)),
         ],
         name="product",
-    )(sidx, pall, sall)
+    )(pairs, table, pall, sall)
     return dens.reshape(1, 1, 8, B, B), product.reshape(1, 1, 8, B, B)
 
 

time: 81.5 us -> 81.3 us (level)
  no operation moved by 1% of the time
where the time goes in v6:
time: 81.3 us; the launch traced here: 81 us
  Pallas kernels  78.4 us (96%)
  between operations  2.58 us (3%)
    pallas_call x1, Pallas kernels, on_device(): pl.pallas_call(gather_kernel, out_shape=(gathered, gathered, jax.ShapeDty...  74.5 us
    pallas_call x1, Pallas kernels, on_device(): pl.pallas_call(product_kernel, out_shape=(jax.ShapeDtypeStruct((8, B, B),...  3.94 us

profile of v6, /device:TPU:1, one launch (start us, length us, event | category | flops | bytes accessed | tf_op | source)
XLA Modules:
  0.0 81.0 jit_solution(14508799958965303222)
XLA Ops:
  2.6 74.5 %gather.1 = (bf16[16,8,128,128]{3,2,1,0:T(8,128)(2,1)}, bf16[16,8,128,128]{3,2,1,0:T(8,128)(2,1)}, s32[8,128]{1,0:T(8,128)}, s32[16,128]{1,0:T(8,128)}) custom-call(bf16[8,128,2048]{2,1,0:T(8,128)(2,1)} %bitcast.13, bf16[8,128,128]{2,1,0:T(8,128)(2,1)} %bitcast.14, s32[8]{0:T(128)} %bitcast.15, s32[1]{0:T(128)} %bitcast.10.p_count_in, s32[8]{0:T(128)} %bitcast.16, ...), custom_call_target="tpu_custom_call" | custom-call | tf_op jit(solution)/shard_map/gather/pallas_call | solution.py:590
  77.1 3.9 %product.1 = (f32[8,128,128]{2,1,0:T(8,128)}, bf16[8,128,128]{2,1,0:T(8,128)(2,1)}) custom-call(s32[8,128]{1,0:T(8,128)} %get-tuple-element.8.pairs, s32[16,128]{1,0:T(8,128)} %get-tuple-element.9.table, bf16[16,8,128,128]{3,2,1,0:T(8,128)(2,1)} %get-tuple-element.10.pall, bf16[16,8,128,128]{3,2,1,0:T(8,128)(2,1)} %get-tuple-element.11.sall), custom_call_target="tpu_custom_call" | custom-call | tf_op jit(solution)/shard_map/product/pallas_call | solution.py:619

commit v7 on v6

--- a/solution.py
+++ b/solution.py
@@ -482,11 +482,15 @@
         pl.when(piece.peer != col)(functools.partial(left, far_send))
 
 
-def product_kernel(pairs, table, pall, sall, out, dens, sidx, todo, pbuf, sbuf, count, sem, sem_p, sem_s):
+def product_kernel(pairs_in, table, pall, sall, out, dens, pairs, held, sidx, todo, pbuf, sbuf, count, sem, sem_p, sem_s):
     depth = pbuf.shape[0]
     col = lax.axis_index("col")
-    keep = pltpu.make_async_copy(pall.at[col], dens, sem.at[0])
-    keep.start()
+    fetch_pairs = pltpu.make_async_copy(pairs_in, pairs, sem.at[2])
+    fetch_pairs.start()
+    take = pltpu.make_async_copy(pall.at[col], held, sem.at[0])
+    take.start()
+    out[...] = jnp.zeros_like(out)
+    fetch_pairs.wait()
     total = pairs[1, 72]
     count[0] = total
 
@@ -555,7 +559,9 @@
         lax.fori_loop(0, 16, tile, 0)
 
     n = count[0]
-    out[...] = jnp.zeros_like(out)
+    take.wait()
+    keep = pltpu.make_async_copy(held, dens, sem.at[3])
+    keep.start()
 
     def work(first, size):
         sums = []
@@ -582,7 +588,6 @@
 def on_device(coeffs, p_slots, p_count, s_blocks, s_slots, s_count, q_slots, q_count):
     rows, orbitals = coeffs.shape
     n = 16
-    smem = pl.BlockSpec(memory_space=pltpu.SMEM)
     vmem = pl.BlockSpec(memory_space=pltpu.VMEM)
     anyspace = pl.BlockSpec(memory_space=pl.ANY)
     gathered = jax.ShapeDtypeStruct((n, rows // B, B, B), jnp.bfloat16)
@@ -621,15 +626,17 @@
         out_shape=(
             jax.ShapeDtypeStruct((8, B, B), jnp.float32), jax.ShapeDtypeStruct((8, B, B), jnp.bfloat16)
         ),
-        in_specs=[smem, anyspace, anyspace, anyspace],
-        out_specs=(vmem, vmem),
+        in_specs=[anyspace, anyspace, anyspace, anyspace],
+        out_specs=(vmem, anyspace),
         scratch_shapes=[
+            pltpu.SMEM((8, B), jnp.int32),
+            pltpu.VMEM((8, B, B), jnp.bfloat16),
             pltpu.SMEM((n, B), jnp.int32),
             pltpu.SMEM((1024,), jnp.int32),
             pltpu.VMEM((depth, B, B), jnp.bfloat16),
             pltpu.VMEM((depth, B, B), jnp.bfloat16),
             pltpu.SMEM((1,), jnp.int32),
-            dma((2,)), dma((depth,)), dma((depth,)),
+            dma((4,)), dma((depth,)), dma((depth,)),
         ],
         name="product",
     )(pairs, table, pall, sall)

time: 81.3 us -> 80.7 us (level)
  no operation moved by 1% of the time
where the time goes in v7:
time: 80.7 us; the launch traced here: 80.6 us
  Pallas kernels  78 us (97%)
  between operations  2.58 us (3%)
    pallas_call x1, Pallas kernels, on_device(): pl.pallas_call(gather_kernel, out_shape=(gathered, gathered, jax.ShapeDty...  74.5 us
    pallas_call x1, Pallas kernels, on_device(): pl.pallas_call(product_kernel, out_shape=(jax.ShapeDtypeStruct((8, B, B),...  3.55 us

profile of v7, /device:TPU:1, one launch (start us, length us, event | category | flops | bytes accessed | tf_op | source)
XLA Modules:
  0.0 80.6 jit_solution(13388621933768335819)
XLA Ops:
  2.6 74.5 %gather.1 = (bf16[16,8,128,128]{3,2,1,0:T(8,128)(2,1)}, bf16[16,8,128,128]{3,2,1,0:T(8,128)(2,1)}, s32[8,128]{1,0:T(8,128)}, s32[16,128]{1,0:T(8,128)}) custom-call(bf16[8,128,2048]{2,1,0:T(8,128)(2,1)} %bitcast.13, bf16[8,128,128]{2,1,0:T(8,128)(2,1)} %bitcast.14, s32[8]{0:T(128)} %bitcast.15, s32[1]{0:T(128)} %bitcast.10.p_count_in, s32[8]{0:T(128)} %bitcast.16, ...), custom_call_target="tpu_custom_call" | custom-call | tf_op jit(solution)/shard_map/gather/pallas_call | solution.py:595
  77.1 3.5 %product.1 = (f32[8,128,128]{2,1,0:T(8,128)}, bf16[8,128,128]{2,1,0:T(8,128)(2,1)}) custom-call(s32[8,128]{1,0:T(8,128)} %get-tuple-element.8.pairs_in, s32[16,128]{1,0:T(8,128)} %get-tuple-element.9.table, bf16[16,8,128,128]{3,2,1,0:T(8,128)(2,1)} %get-tuple-element.10.pall, bf16[16,8,128,128]{3,2,1,0:T(8,128)(2,1)} %get-tuple-element.11.sall), custom_call_target="tpu_custom_call" | custom-call | tf_op jit(solution)/shard_map/product/pallas_call | solution.py:624
